TPU v7x, 8 devices: a whole 2x2x1 slice. The times are simulated.
8 devices in a mesh: pp: 4 (over z, y, x), ep: 2 (over core).
Axes of the slice: x: 2, y: 2, z: 1, core: 2. Of those that a mesh axis runs over, the one named last changes fastest.
Arguments:
- expert_out: bfloat16 [8, 128, 48, 4096], P('pp', 'ep')
- expert_ids: int32 [8, 4, 128, 8], P('pp', 'ep')
- slot_ids: int32 [8, 4, 128, 8], P('pp', 'ep')
- gate_vals: float32 [8, 4, 128, 8], P('pp', 'ep')
- residual: bfloat16 [8, 4, 128, 4096], P('pp', 'ep')
- norm_w: float32 [4, 4096], P('pp')
- w_query: bfloat16 [4, 4096, 64, 128], P('pp')
- w_key: bfloat16 [4, 4096, 64, 128], P('pp')
- w_value: bfloat16 [4, 4096, 64, 128], P('pp')
- w_out: bfloat16 [4, 64, 128, 4096], P('pp')
Outputs:
- output: bfloat16 [8, 4, 128, 4096], P('pp', 'ep')
All inputs are finite; a program needn't handle non-finite values.
Results may differ from a plain program's by a relative error of at most 0.0139631.
Values are sent between devices in bfloat16 or wider.
A program may use at most 1.25 GiB of HBM per device.

v0:
```python
import jax
import jax.numpy as jnp
from jax import lax
from jax.sharding import PartitionSpec as P

NORM_EPS = 1e-6


def gated_sum(exp_table, expert_ids, slot_pos, gate_vals, residual):
    is_kept = slot_pos >= 0
    pick_rows = jax.vmap(lambda exp_rows, id_blk, pos_blk: exp_rows[id_blk, pos_blk])
    picked = pick_rows(exp_table, expert_ids, jnp.where(is_kept, slot_pos, 0))
    weight = jnp.where(is_kept, gate_vals, 0.0)
    mixed_sum = residual.astype(jnp.float32) + jnp.sum(weight[..., None] * picked.astype(jnp.float32), axis=3)
    return mixed_sum.astype(jnp.bfloat16)


def attention_block(combined, norm_w, w_query, w_key, w_value, w_out):
    y_wide = combined.astype(jnp.float32)
    inv_rms = lax.rsqrt(jnp.mean(y_wide * y_wide, axis=-1, keepdims=True) + NORM_EPS)
    x_in = (y_wide * inv_rms * norm_w).astype(jnp.bfloat16)
    q_heads = jnp.einsum('bld,dhe->blhe', x_in, w_query, preferred_element_type=jnp.float32).astype(jnp.bfloat16)
    k_heads = jnp.einsum('bld,dhe->blhe', x_in, w_key, preferred_element_type=jnp.float32).astype(jnp.bfloat16)
    v_heads = jnp.einsum('bld,dhe->blhe', x_in, w_value, preferred_element_type=jnp.float32).astype(jnp.bfloat16)
    head_dim = w_query.shape[2]
    seq_len = combined.shape[1]
    scores = jnp.einsum('bqhe,bkhe->bhqk', q_heads, k_heads, preferred_element_type=jnp.float32) * (head_dim ** -0.5)
    causal = jnp.arange(seq_len)[:, None] >= jnp.arange(seq_len)[None, :]
    attn_probs = jax.nn.softmax(jnp.where(causal, scores, -jnp.inf), axis=-1).astype(jnp.bfloat16)
    attn_out = jnp.einsum('bhqk,bkhe->bqhe', attn_probs, v_heads, preferred_element_type=jnp.float32).astype(jnp.bfloat16)
    out_proj = jnp.einsum('crif,ife->cre', attn_out, w_out, preferred_element_type=jnp.float32).astype(jnp.bfloat16)
    return (y_wide + out_proj.astype(jnp.float32)).astype(jnp.bfloat16)


def solution(mesh):
    stages = mesh.shape['pp']
    group_size = mesh.shape['ep']
    send_next = [(src_row, (src_row + 1) % stages) for src_row in range(stages)]
    tok_spec = P('pp', 'ep', None, None)
    wt_spec = P('pp', None, None, None)

    def device_step(expert_out, expert_ids, slot_ids, gate_vals, residual, norm_w, w_query, w_key, w_value, w_out):
        num_micro, seqs_dev, seq_len, d_model = residual.shape
        src_slots = expert_out.shape[2] // group_size
        returned = lax.all_to_all(expert_out, 'ep', 2, 1, tiled=True)
        block_base = lax.axis_index('ep') * src_slots
        slot_pos = jnp.where(slot_ids >= 0, slot_ids - block_base, -1)
        combined = gated_sum(returned, expert_ids, slot_pos, gate_vals, residual)
        arrived = lax.ppermute(combined, 'pp', send_next)
        flat_in = arrived.reshape(num_micro * seqs_dev, seq_len, d_model)
        result = attention_block(flat_in, norm_w[0], w_query[0], w_key[0], w_value[0], w_out[0])
        return result.reshape(num_micro, seqs_dev, seq_len, d_model)

    return jax.shard_map(device_step, mesh=mesh, in_specs=(tok_spec, tok_spec, tok_spec, tok_spec, tok_spec, P('pp', None), wt_spec, wt_spec, wt_spec, wt_spec), out_specs=tok_spec, check_vma=False)
```

profile of v0, /device:TPU:0, one launch (start us, length us, event | category | flops | bytes accessed | tf_op | source)
XLA Modules:
  0.0 651.8 jit_solution(6640577565520795239)
XLA Ops:
  0.0 42.7 %copy.17 = bf16[2,64,48,4096]{3,1,0,2:T(8,128)(2,1)} copy(bf16[2,64,48,4096]{3,2,1,0:T(8,128)(2,1)} %param.10) | data formatting | bytes 100663296 | tf_op args[0]
  42.7 0.0 copy-start.1
  42.7 0.0 copy-start.3
  42.8 19.3 %all-to-all-start = ((bf16[2,64,48,4096]{3,1,0,2:T(8,128)(2,1)}), bf16[2,64,48,4096]{3,1,0,2:T(8,128)(2,1)}, u32[]{:S(2)}, u32[]{:S(2)}) async-start(bf16[2,64,48,4096]{3,1,0,2:T(8,128)(2,1)} %copy.17), calls=%async_computation | async-start | bytes 100663296 | tf_op jit(solution)/shard_map/all_to_all | solution.py:45
  62.0 0.0 copy-done.1
  62.1 0.0 copy-done.3
  62.1 0.1 copy.19
  62.2 0.2 reshape.32
  62.4 37.1 %all-to-all-done = bf16[2,64,48,4096]{3,1,0,2:T(8,128)(2,1)} async-done(((bf16[2,64,48,4096]{3,1,0,2:T(8,128)(2,1)}), bf16[2,64,48,4096]{3,1,0,2:T(8,128)(2,1)}, u32[]{:S(2)}, u32[]{:S(2)}) %all-to-all-start) | async-done | bytes 50331680 | tf_op jit(solution)/shard_map/all_to_all | solution.py:45
  99.5 0.0 copy-start.4
  99.5 43.1 %copy.18 = bf16[2,64,2,24,4096]{4,3,1,2,0:T(8,128)(2,1)} copy(bf16[2,64,2,24,4096]{4,1,0,3,2:T(8,128)(2,1)} %bitcast) | data formatting | bytes 100663296 | tf_op jit(solution)/shard_map/all_to_all | solution.py:45
  142.5 0.0 copy-done.4
  142.6 0.1 copy.16
  142.7 148.7 %gather_fusion = bf16[4096,4096]{1,0:T(8,128)(2,1)} fusion(bf16[2,128,24,4096]{3,2,1,0:T(8,128)(2,1)} %bitcast.91, s32[4096]{0:T(1024)S(1)} %reshape.32), kind=kCustom, calls=%fused_computation | custom fusion | bytes 67158016 | tf_op jit(solution)/shard_map/vmap()/gather | solution.py:11
  291.4 32.6 %fusion.1 = f32[2,2,128,4096]{3,2,1,0:T(8,128)} fusion(f32[2,2,128,8]{3,2,1,0:T(8,128)S(1)} %copy.16, bf16[4096,4096]{1,0:T(8,128)(2,1)} %gather_fusion), kind=kLoop, calls=%fused_computation.3 | loop fusion | flops 48234496 | bytes 41959424 | tf_op jit(solution)/shard_map/reduce_sum | solution.py:14
  324.0 0.0 copy-start.2
  324.0 5.9 add_convert_fusion
  329.9 8.6 %collective-permute-start = (bf16[2,2,128,4096]{3,2,1,0:T(8,128)(2,1)S(1)}, bf16[2,2,128,4096]{3,2,1,0:T(8,128)(2,1)S(1)}, u32[]{:S(2)}, u32[]{:S(2)}) collective-permute-start(bf16[2,2,128,4096]{3,2,1,0:T(8,128)(2,1)S(1)} %add_convert_fusion), channel_id=1, source_target_pairs={{0,2},{2,4},{4,6},{6,0},{1,3},{3,5},{5,7},{7,1}} | collective-permute-start | bytes 12582920 | tf_op jit(solution)/shard_map/ppermute | solution.py:49
  338.5 0.6 iota_compare_fusion
  339.1 89.7 %collective-permute-done = bf16[2,2,128,4096]{3,2,1,0:T(8,128)(2,1)S(1)} collective-permute-done((bf16[2,2,128,4096]{3,2,1,0:T(8,128)(2,1)S(1)}, bf16[2,2,128,4096]{3,2,1,0:T(8,128)(2,1)S(1)}, u32[]{:S(2)}, u32[]{:S(2)}) %collective-permute-start) | collective-permute-done | bytes 4194336 | tf_op jit(solution)/shard_map/ppermute | solution.py:49
  428.8 0.0 copy-start
  428.8 0.9 multiply_reduce_fusion
  429.7 1.0 copy-done
  430.7 0.0 copy-done.2
  430.7 1.6 multiply_convert_fusion
  432.3 41.0 %fusion.4 = bf16[4,128,64,128]{3,1,2,0:T(8,128)(2,1)} fusion(bf16[4,128,4096,1]{2,1,3,0:T(8,128)(2,1)S(1)} %bitcast.92, bf16[4096,64,128]{2,1,0:T(8,128)(2,1)} %bitcast.17), kind=kOutput, calls=%fused_computation.6 | convolution fusion | flops 34359738368 | bytes 79691776 | tf_op jit(solution)/shard_map/bld,dhe->blhe/dot_general | solution.py:23
  473.3 40.8 %fusion.83 = bf16[4,128,64,128]{3,1,2,0:T(8,128)(2,1)} fusion(bf16[4,128,4096,1]{2,1,3,0:T(8,128)(2,1)S(1)} %bitcast.93, bf16[4096,64,128]{2,1,0:T(8,128)(2,1)} %bitcast.15), kind=kOutput, calls=%fused_computation.30.clone.1 | convolution fusion | flops 34363932672 | bytes 79691776 | tf_op jit(solution)/shard_map/bld,dhe->blhe/dot_general | solution.py:22
  514.1 41.0 %fusion.8 = bf16[4,128,64,128]{3,1,2,0:T(8,128)(2,1)} fusion(bf16[4,128,4096,1]{2,1,3,0:T(8,128)(2,1)S(1)} %bitcast.94, bf16[4096,64,128]{2,1,0:T(8,128)(2,1)} %bitcast.11), kind=kOutput, calls=%fused_computation.10 | convolution fusion | flops 34359738368 | bytes 79691776 | tf_op jit(solution)/shard_map/bld,dhe->blhe/dot_general | solution.py:24
  555.2 0.0 copy-start.5
  555.2 17.4 %fusion.22 = f32[4,64,128,128]{2,3,1,0:T(8,128)} fusion(bf16[4,128,64,128]{3,1,2,0:T(8,128)(2,1)} %fusion.4, bf16[4,128,64,128]{3,1,2,0:T(8,128)(2,1)} %fusion.83), kind=kOutput, calls=%fused_computation.28 | convolution fusion | flops 1073741824 | bytes 33554432 | tf_op jit(solution)/shard_map/bqhe,bkhe->bhqk/dot_general | solution.py:27
  572.6 0.0 copy-done.5
  572.6 15.4 %fusion.60 = f32[4,64,128]{2,1,0:T(8,128)S(1)} fusion(f32[4,64,128,128]{2,3,1,0:T(8,128)} %fusion.22, pred[128,128]{0,1:T(8,128)(4,1)S(1)} %copy-done.5), kind=kOutput, calls=%fused_computation.55 | output fusion | flops 25165952 | bytes 16924672 | tf_op jit(solution)/shard_map/sub | solution.py:29
  588.0 18.8 %fusion.79 = bf16[4,128,64,128]{1,3,2,0:T(8,128)(2,1)} fusion(f32[4,64,128]{2,1,0:T(8,128)S(1)} %fusion.60, bf16[4,128,64,128]{3,1,2,0:T(8,128)(2,1)} %fusion.8, f32[4,64,128,128]{2,3,1,0:T(8,128)} %fusion.22, pred[128,128]{0,1:T(8,128)(4,1)S(1)} %copy-done.5), kind=kOutput, calls=%fused_computation.21.clone.clone.clone.clone.clone.1 | convolution fusion | flops 1107329152 | bytes 33701888 | tf_op jit(solution)/shard_map/bhqk,bkhe->bqhe/dot_general | solution.py:30
  606.7 44.8 %fusion.16 = bf16[4,128,4096]{2,1,0:T(8,128)(2,1)} fusion(bf16[1,64,128,4096]{3,2,1,0:T(8,128)(2,1)} %param.19, bf16[2,2,128,4096]{3,2,1,0:T(8,128)(2,1)} %copy-done, bf16[4,128,64,128]{1,3,2,0:T(8,128)(2,1)} %fusion.79), kind=kOutput, calls=%fused_computation.23 | convolution fusion | flops 34370224128 | bytes 83886080 | tf_op jit(solution)/shard_map/crif,ife->cre/dot_general | solution.py:31
  (3 shorter events, 0.0 us)
Async XLA Ops:
  42.7 19.3 %copy-start.1 = (s32[2,2,128,8]{2,3,1,0:T(8,128)S(1)}, s32[2,2,128,8]{2,3,1,0:T(8,128)}, u32[]{:S(2)}) copy-start(s32[2,2,128,8]{2,3,1,0:T(8,128)} %param.12) | copy-start | bytes 49156
  42.7 19.3 %copy-start.3 = (s32[2,2,128,8]{2,3,1,0:T(8,128)S(1)}, s32[2,2,128,8]{2,3,1,0:T(8,128)}, u32[]{:S(2)}) copy-start(s32[2,2,128,8]{2,3,1,0:T(8,128)} %param.11) | copy-start | bytes 49156
  42.8 56.7 %all-to-all-start = ((bf16[2,64,48,4096]{3,1,0,2:T(8,128)(2,1)}), bf16[2,64,48,4096]{3,1,0,2:T(8,128)(2,1)}, u32[]{:S(2)}, u32[]{:S(2)}) async-start(bf16[2,64,48,4096]{3,1,0,2:T(8,128)(2,1)} %copy.17), calls=%async_computation | async-start | bytes 100663296 | tf_op jit(solution)/shard_map/all_to_all | solution.py:45
  99.5 43.1 %copy-start.4 = (f32[2,2,128,8]{2,3,1,0:T(8,128)S(1)}, f32[2,2,128,8]{2,3,1,0:T(8,128)}, u32[]{:S(2)}) copy-start(f32[2,2,128,8]{2,3,1,0:T(8,128)} %param.13) | copy-start | bytes 49156
  324.0 106.7 %copy-start.2 = (f32[1,4096]{1,0:T(1,128)S(1)}, f32[1,4096]{1,0:T(1,128)}, u32[]{:S(2)}) copy-start(f32[1,4096]{1,0:T(1,128)} %param.15) | copy-start | bytes 49156
  329.9 98.9 %collective-permute-start = (bf16[2,2,128,4096]{3,2,1,0:T(8,128)(2,1)S(1)}, bf16[2,2,128,4096]{3,2,1,0:T(8,128)(2,1)S(1)}, u32[]{:S(2)}, u32[]{:S(2)}) collective-permute-start(bf16[2,2,128,4096]{3,2,1,0:T(8,128)(2,1)S(1)} %add_convert_fusion), channel_id=1, source_target_pairs={{0,2},{2,4},{4,6},{6,0},{1,3},{3,5},{5,7},{7,1}} | collective-permute-start | bytes 12582920 | tf_op jit(solution)/shard_map/ppermute | solution.py:49
  428.8 1.9 copy-start
  555.2 17.4 %copy-start.5 = (pred[128,128]{0,1:T(8,128)(4,1)S(1)}, pred[128,128]{0,1:T(8,128)(4,1)}, u32[]{:S(2)}) copy-start(pred[128,128]{0,1:T(8,128)(4,1)} %iota_compare_fusion) | copy-start | bytes 49156
where the time goes:
time: 659 us; the launch traced here: 652 us
  local copies, waits for them, and re-layouts  236 us (36%)
  matrix products  204 us (31%)
  waiting for transfers between devices  127 us (19%)
  other arithmetic  57 us (9%)
  starting transfers between devices  27.9 us (4%)
    gather x3, local copies, waits for them, and re-layouts, gated_sum(): exp_rows[id_blk, pos_blk]  149 us
    ppermute x1, waiting for transfers between devices, device_step(): arrived = lax.ppermute(combined, 'pp', send_next)  89.7 us
    dot_general x1, matrix products, attention_block(): jnp.einsum('crif,ife->cre', attn_out, w_out, preferred_element_type=jnp.f...  44.8 us
    unnamed x13, local copies, waits for them, and re-layouts  43.8 us
    all_to_all x1, local copies, waits for them, and re-layouts, device_step(): returned = lax.all_to_all(expert_out, 'ep', 2, 1, tiled=True)  43.1 us
    dot_general x1, matrix products, attention_block(): jnp.einsum('bld,dhe->blhe', x_in, w_value, preferred_element_type=jnp.flo...  41 us
    dot_general x1, matrix products, attention_block(): jnp.einsum('bld,dhe->blhe', x_in, w_key, preferred_element_type=jnp.float32)  41 us
    dot_general x1, matrix products, attention_block(): jnp.einsum('bld,dhe->blhe', x_in, w_query, preferred_element_type=jnp.flo...  40.8 us
  transfers between devices with their start and end apart: 2, of which 2 were waited for; matrix products, arithmetic and copies ran while one was open for 0% of the time, Pallas kernels for 0%

commit v1 on v0

v1 whole, which is shorter than its diff:
```python
import functools

import jax
import jax.numpy as jnp
from jax import lax
from jax.experimental import pallas as pl
from jax.experimental.pallas import tpu as pltpu
from jax.sharding import PartitionSpec as P


NORM_EPS = 1e-6
COL = 512


def split_gate(full):
    hi = full.astype(jnp.bfloat16)
    rest = full - hi.astype(jnp.float32)
    mid = rest.astype(jnp.bfloat16)
    lo = (rest - mid.astype(jnp.float32)).astype(jnp.bfloat16)
    return hi, mid, lo


def mix_kernel(has_add, side_ref, code_ref, gate_ref, exp_ref, *rest):
    if has_add:
        res_ref, part_ref, out_ref, w_ref = rest
    else:
        out_ref, w_ref = rest
    tokens, top_k = code_ref.shape
    slots = w_ref.shape[2]

    @pl.when(pl.program_id(0) == 0)
    def build():
        for t0 in range(0, tokens, 64):
            code = code_ref[t0:t0 + 64, :]
            gate = gate_ref[t0:t0 + 64, :]
            for s0 in range(0, slots, 512):
                lane = lax.broadcasted_iota(jnp.int32, (64, 512), 1) + s0
                full = jnp.zeros((64, 512), jnp.float32)
                for i in range(top_k):
                    full = jnp.where(lane == code[:, i:i + 1], gate[:, i:i + 1], full)
                for part, val in enumerate(split_gate(full)):
                    w_ref[part, t0:t0 + 64, s0:s0 + 512] = val

    exp_rows = exp_ref[0].reshape(slots, exp_ref.shape[3])
    total = jnp.dot(w_ref[0], exp_rows, preferred_element_type=jnp.float32)
    total += jnp.dot(w_ref[1], exp_rows, preferred_element_type=jnp.float32)
    total += jnp.dot(w_ref[2], exp_rows, preferred_element_type=jnp.float32)
    if has_add:
        total = total + part_ref[...] + res_ref[...].astype(jnp.float32)
    out_ref[...] = total.astype(out_ref.dtype)


def mix(expert_out, row, side, code, gate, add=None):
    tokens, top_k = code.shape
    _, experts, cap, d_model = expert_out.shape
    half = cap // 2
    small = pl.BlockSpec((tokens, top_k), lambda c, s: (0, 0))
    cols = pl.BlockSpec((tokens, COL), lambda c, s: (0, c))
    in_specs = [small, small, pl.BlockSpec((1, experts, half, COL), lambda c, s: (row, 0, s[0], c))]
    args = [code, gate, expert_out]
    if add is not None:
        in_specs += [cols, cols]
        args += list(add)
    slots = experts * half
    return pl.pallas_call(
        functools.partial(mix_kernel, add is not None),
        out_shape=jax.ShapeDtypeStruct((tokens, d_model), jnp.float32 if add is None else jnp.bfloat16),
        grid_spec=pltpu.PrefetchScalarGridSpec(
            num_scalar_prefetch=1,
            grid=(d_model // COL,),
            in_specs=in_specs,
            out_specs=cols,
            scratch_shapes=[pltpu.VMEM((3, tokens, slots), jnp.bfloat16)],
        ),
        cost_estimate=pl.CostEstimate(flops=6 * tokens * slots * d_model, bytes_accessed=2 * slots * d_model, transcendentals=0),
    )(side.reshape(1), *args)


def attn_kernel(seq_len, q_ref, k_ref, v_ref, o_ref):
    heads, tokens, head_dim = q_ref.shape
    row = lax.broadcasted_iota(jnp.int32, (seq_len, seq_len), 0)
    col = lax.broadcasted_iota(jnp.int32, (seq_len, seq_len), 1)
    causal = row >= col
    for h in range(heads):
        for t0 in range(0, tokens, seq_len):
            q = q_ref[h, t0:t0 + seq_len, :]
            k = k_ref[h, t0:t0 + seq_len, :]
            v = v_ref[h, t0:t0 + seq_len, :]
            scores = lax.dot_general(q, k, (((1,), (1,)), ((), ())), preferred_element_type=jnp.float32) * (head_dim ** -0.5)
            scores = jnp.where(causal, scores, -jnp.inf)
            expd = jnp.exp(scores - jnp.max(scores, axis=1, keepdims=True))
            probs = (expd / jnp.sum(expd, axis=1, keepdims=True)).astype(jnp.bfloat16)
            out = jnp.dot(probs, v, preferred_element_type=jnp.float32).astype(jnp.bfloat16)
            o_ref[t0:t0 + seq_len, h * head_dim:(h + 1) * head_dim] = out


def attention(q, k, v, seq_len):
    heads, tokens, head_dim = q.shape
    group = 8
    spec = pl.BlockSpec((group, tokens, head_dim), lambda g: (g, 0, 0))
    return pl.pallas_call(
        functools.partial(attn_kernel, seq_len),
        out_shape=jax.ShapeDtypeStruct((tokens, heads * head_dim), jnp.bfloat16),
        grid=(heads // group,),
        in_specs=[spec] * 3,
        out_specs=pl.BlockSpec((tokens, group * head_dim), lambda g: (0, g)),
        cost_estimate=pl.CostEstimate(flops=16 * tokens * seq_len * heads * head_dim, bytes_accessed=8 * tokens * heads * head_dim, transcendentals=tokens * seq_len * heads),
    )(q, k, v)


def attention_block(combined, seq_len, norm_w, w_query, w_key, w_value, w_out):
    y_wide = combined.astype(jnp.float32)
    inv_rms = lax.rsqrt(jnp.mean(y_wide * y_wide, axis=-1, keepdims=True) + NORM_EPS)
    x_in = (y_wide * inv_rms * norm_w).astype(jnp.bfloat16)
    heads = []
    for w in (w_query, w_key, w_value):
        heads.append(jnp.einsum('td,dhe->hte', x_in, w, preferred_element_type=jnp.float32).astype(jnp.bfloat16))
    attn_out = attention(*heads, seq_len)
    w_flat = w_out.reshape(-1, w_out.shape[-1])
    out_proj = jnp.dot(attn_out, w_flat, preferred_element_type=jnp.float32).astype(jnp.bfloat16)
    return (y_wide + out_proj.astype(jnp.float32)).astype(jnp.bfloat16)


def solution(mesh):
    stages = mesh.shape['pp']
    send_next = [(src_row, (src_row + 1) % stages) for src_row in range(stages)]
    swap = [(0, 1), (1, 0)]
    tok_spec = P('pp', 'ep', None, None)
    wt_spec = P('pp', None, None, None)

    def step(expert_out, expert_ids, slot_ids, gate_vals, residual, norm_w, w_query, w_key, w_value, w_out):
        num_micro, seqs_dev, seq_len, d_model = residual.shape
        experts, cap = expert_out.shape[1:3]
        half = cap // 2
        tokens = seqs_dev * seq_len
        me = lax.axis_index('ep').astype(jnp.int32)
        code = jnp.where(slot_ids >= 0, expert_ids * half + slot_ids - me * half, -1)
        theirs = lax.ppermute(jnp.stack([code.astype(jnp.float32), gate_vals]), 'ep', swap)
        code = code.reshape(num_micro, tokens, -1)
        gate = gate_vals.reshape(num_micro, tokens, -1)
        their_code = theirs[0].astype(jnp.int32).reshape(num_micro, tokens, -1)
        their_gate = theirs[1].reshape(num_micro, tokens, -1)
        first = me * experts * half
        flat_h = residual.reshape(num_micro, tokens, d_model)
        arrived = []
        for m in range(num_micro):
            part = mix(expert_out, m, 1 - me, their_code[m] - first, their_gate[m])
            got = lax.ppermute(part, 'ep', swap)
            y = mix(expert_out, m, me, code[m] - first, gate[m], (flat_h[m], got))
            arrived.append(lax.ppermute(y, 'pp', send_next))
        outs = [attention_block(y, seq_len, norm_w[0], w_query[0], w_key[0], w_value[0], w_out[0]) for y in arrived]
        return jnp.stack(outs).reshape(num_micro, seqs_dev, seq_len, d_model)

    return jax.shard_map(step, mesh=mesh, in_specs=(tok_spec, tok_spec, tok_spec, tok_spec, tok_spec, P('pp', None), wt_spec, wt_spec, wt_spec, wt_spec), out_specs=tok_spec, check_vma=False)
```

time: 659 us -> 564 us (0.86)
  local copies, waits for them, and re-layouts: 236 us -> 12.3 us
  Pallas kernels: 0 us -> 153 us
  matrix products: 204 us -> 302 us
  waiting for transfers between devices: 127 us -> 74.5 us
  other arithmetic: 57 us -> 6.47 us
  starting transfers between devices: 27.9 us -> 5.66 us
    pallas_call x0 -> x6, Pallas kernels: none -> 153 us  [the longest x2 88.5 us: attention(): pl.pallas_call(functools.partial(attn_kernel, seq_len), out_shape=jax.Sha...]
    gather x3 -> x0, local copies, waits for them, and re-layouts: 149 us -> none  [gated_sum(): exp_rows[id_blk, pos_blk]]
    dot_general x6 -> x8, matrix products: 204 us -> 302 us  [the longest x6 245 us: attention_block(): jnp.einsum('td,dhe->hte', x_in, w, preferred_element_type=jnp.float32)]
    all_to_all x1 -> x0, local copies, waits for them, and re-layouts: 43.1 us -> none  [device_step(): returned = lax.all_to_all(expert_out, 'ep', 2, 1, tiled=True)]
    unnamed x13 -> x12, local copies, waits for them, and re-layouts: 43.8 us -> 1.35 us
    all_to_all x1 -> x0, waiting for transfers between devices: 37.1 us -> none  [device_step(): returned = lax.all_to_all(expert_out, 'ep', 2, 1, tiled=True)]
    reduce_sum x1 -> x0, other arithmetic: 32.6 us -> none  [gated_sum(): jnp.sum(weight[..., None] * picked.astype(jnp.float32), axis=3)]
    all_to_all x1 -> x0, starting transfers between devices: 19.3 us -> none  [device_step(): returned = lax.all_to_all(expert_out, 'ep', 2, 1, tiled=True)]
  transfers between devices with their start and end apart: 2 -> 5, of which waited for: 2 -> 3; matrix products, arithmetic and copies ran while one was open for 0% -> 2% of each run, Pallas kernels for 0% -> 9%
where the time goes in v1:
time: 564 us; the launch traced here: 554 us
  matrix products  302 us (54%)
  Pallas kernels  153 us (27%)
  waiting for transfers between devices  74.5 us (13%)
  local copies, waits for them, and re-layouts  12.3 us (2%)
  other arithmetic  6.47 us (1%)
  starting transfers between devices  5.66 us (1%)
    dot_general x6, matrix products, attention_block(): jnp.einsum('td,dhe->hte', x_in, w, preferred_element_type=jnp.float32)  245 us
    pallas_call x2, Pallas kernels, attention(): pl.pallas_call(functools.partial(attn_kernel, seq_len), out_shape=jax.Sha...  88.5 us
    ppermute x2, waiting for transfers between devices, step(): arrived.append(lax.ppermute(y, 'pp', send_next))  73.6 us
    pallas_call x4, Pallas kernels, mix(): pl.pallas_call(functools.partial(mix_kernel, add is not None), out_shape=...  64.9 us
    dot_general x2, matrix products, attention_block(): jnp.dot(attn_out, w_flat, preferred_element_type=jnp.float32)  56.8 us
  transfers between devices with their start and end apart: 5, of which 3 were waited for; matrix products, arithmetic and copies ran while one was open for 2% of the time, Pallas kernels for 9%

profile of v1, /device:TPU:0, one launch (start us, length us, event | category | flops | bytes accessed | tf_op | source)
XLA Modules:
  0.0 554.3 jit_solution(7465335392413234526)
XLA Ops:
  0.0 0.7 convert_bitcast_fusion.6
  0.7 0.7 pad_maximum_fusion.1
  1.5 0.8 collective-permute-start
  2.3 0.9 collective-permute-done
  3.2 0.8 copy.13
  4.0 0.8 copy.14
  4.8 16.0 %shard_map.100 = f32[256,4096]{1,0:T(8,128)} custom-call(s32[1]{0:T(128)} %bitcast.4.side_ref, s32[256,8]{1,0:T(8,128)} %bitcast.56, f32[256,8]{1,0:T(8,128)} %bitcast.59, bf16[2,64,48,4096]{3,2,1,0:T(8,128)(2,1)} %exp_ref.7), custom_call_target="tpu_custom_call" | custom-call | flops 9663676416 | bytes 12582912 | tf_op jit(solution)/shard_map/pallas_call | solution.py:65
  20.8 0.3 collective-permute-start.1
  21.1 0.8 copy.17
  21.9 0.8 copy.18
  22.7 0.0 copy-start.4
  22.7 16.0 %shard_map.103 = f32[256,4096]{1,0:T(8,128)} custom-call(s32[1]{0:T(128)} %bitcast.4.side_ref, s32[256,8]{1,0:T(8,128)} %bitcast.57, f32[256,8]{1,0:T(8,128)} %bitcast.58, bf16[2,64,48,4096]{3,2,1,0:T(8,128)(2,1)} %exp_ref.7), custom_call_target="tpu_custom_call" | custom-call | flops 9663676416 | bytes 12582912 | tf_op jit(solution)/shard_map/pallas_call | solution.py:65
  38.7 0.2 collective-permute-start.3
  38.8 0.8 copy.11
  39.6 0.0 copy-done.4
  39.6 0.8 copy.12
  40.4 0.8 copy.15
  41.2 0.8 copy.16
  42.0 4.7 fusion.42
  46.7 0.0 collective-permute-done.1.rest_1_
  46.7 16.5 %shard_map.101 = bf16[256,4096]{1,0:T(8,128)(2,1)} custom-call(s32[1]{0:T(128)} %bitcast.side_ref, s32[256,8]{1,0:T(8,128)} %bitcast.54, f32[256,8]{1,0:T(8,128)} %bitcast.55, bf16[2,64,48,4096]{3,2,1,0:T(8,128)(2,1)} %exp_ref.7, bf16[256,4096]{1,0:T(8,128)(2,1)} %bitcast.49, f32[256,4096]{1,0:T(8,128)} %collective-permute-done.1.rest_1_), custom_call_target="tpu_custom_call" | custom-call | flops 9663676416 | bytes 12582912 | tf_op jit(solution)/shard_map/pallas_call | solution.py:65
  63.1 2.8 collective-permute-start.2
  66.0 0.0 collective-permute-done.3.rest_1_
  66.0 16.4 %shard_map.104 = bf16[256,4096]{1,0:T(8,128)(2,1)} custom-call(s32[1]{0:T(128)} %bitcast.side_ref, s32[256,8]{1,0:T(8,128)} %bitcast.52, f32[256,8]{1,0:T(8,128)} %bitcast.53, bf16[2,64,48,4096]{3,2,1,0:T(8,128)(2,1)} %exp_ref.7, bf16[256,4096]{1,0:T(8,128)(2,1)} %bitcast.48, f32[256,4096]{1,0:T(8,128)} %collective-permute-done.3.rest_1_), custom_call_target="tpu_custom_call" | custom-call | flops 9663676416 | bytes 12582912 | tf_op jit(solution)/shard_map/pallas_call | solution.py:65
  82.4 0.0 copy-start.5
  82.4 1.5 collective-permute-start.4
  83.9 29.7 %collective-permute-done.2 = bf16[256,4096]{1,0:T(8,128)(2,1)S(1)} collective-permute-done((bf16[256,4096]{1,0:T(8,128)(2,1)}, bf16[256,4096]{1,0:T(8,128)(2,1)S(1)}, u32[]{:S(2)}, u32[]{:S(2)}) %collective-permute-start.2) | collective-permute-done | bytes 2097184 | tf_op jit(solution)/shard_map/ppermute | solution.py:150
  113.6 0.5 fusion.16
  114.1 43.9 %collective-permute-done.4 = bf16[256,4096]{1,0:T(8,128)(2,1)S(1)} collective-permute-done((bf16[256,4096]{1,0:T(8,128)(2,1)}, bf16[256,4096]{1,0:T(8,128)(2,1)S(1)}, u32[]{:S(2)}, u32[]{:S(2)}) %collective-permute-start.4) | collective-permute-done | bytes 2097184 | tf_op jit(solution)/shard_map/ppermute | solution.py:150
  158.0 0.0 copy-start.1
  158.0 1.3 copy-done.1
  159.4 0.5 fusion.19
  159.9 0.0 copy-done.5
  159.9 40.4 %convert_bitcast_fusion.3.v_ref = bf16[64,256,128]{2,1,0:T(8,128)(2,1)} fusion(bf16[4096,64,128]{2,1,0:T(8,128)(2,1)} %bitcast.15, bf16[256,4096]{1,0:T(8,128)(2,1)S(1)} %collective-permute-done.2, f32[4096]{0:T(1024)S(1)} %bitcast.61, f32[256]{0:T(256)S(1)} %add_rsqrt_fusion.1), kind=kOutput, calls=%fused_computation.34 | convolution fusion | flops 17186160640 | bytes 73417728 | tf_op jit(solution)/shard_map/td,dhe->hte/dot_general | solution.py:117
  200.3 40.5 %convert_bitcast_fusion.4.k_ref = bf16[64,256,128]{2,1,0:T(8,128)(2,1)} fusion(bf16[4096,64,128]{2,1,0:T(8,128)(2,1)} %bitcast.13, bf16[256,4096]{1,0:T(8,128)(2,1)S(1)} %collective-permute-done.2, f32[4096]{0:T(1024)S(1)} %bitcast.62, f32[256]{0:T(256)S(1)} %add_rsqrt_fusion.1), kind=kOutput, calls=%fused_computation.35 | convolution fusion | flops 17186160640 | bytes 73417728 | tf_op jit(solution)/shard_map/td,dhe->hte/dot_general | solution.py:117
  240.8 40.8 %convert_bitcast_fusion.5.q_ref = bf16[64,256,128]{2,1,0:T(8,128)(2,1)} fusion(bf16[4096,64,128]{2,1,0:T(8,128)(2,1)} %bitcast.11, bf16[256,4096]{1,0:T(8,128)(2,1)S(1)} %collective-permute-done.2, f32[4096]{0:T(1024)S(1)} %bitcast.63, f32[256]{0:T(256)S(1)} %add_rsqrt_fusion.1), kind=kOutput, calls=%fused_computation.36 | convolution fusion | flops 17186160640 | bytes 73417728 | tf_op jit(solution)/shard_map/td,dhe->hte/dot_general | solution.py:117
  281.6 44.2 %shard_map.102 = bf16[256,8192]{1,0:T(8,128)(2,1)} custom-call(bf16[64,256,128]{2,1,0:T(8,128)(2,1)} %convert_bitcast_fusion.5.q_ref, bf16[64,256,128]{2,1,0:T(8,128)(2,1)} %convert_bitcast_fusion.4.k_ref, bf16[64,256,128]{2,1,0:T(8,128)(2,1)} %convert_bitcast_fusion.3.v_ref), custom_call_target="tpu_custom_call" | custom-call | flops 4294967296 | bytes 16777216 | tf_op jit(solution)/shard_map/pallas_call | solution.py:101
  325.8 40.9 %convert_bitcast_fusion.v_ref = bf16[64,256,128]{2,1,0:T(8,128)(2,1)} fusion(bf16[4096,64,128]{2,1,0:T(8,128)(2,1)} %bitcast.15, bf16[256,4096]{1,0:T(8,128)(2,1)} %copy-done.1, f32[256]{0:T(256)S(1)} %add_rsqrt_fusion, f32[4096]{0:T(1024)S(1)} %bitcast.64), kind=kOutput, calls=%fused_computation.31 | convolution fusion | flops 17186160640 | bytes 73417728 | tf_op jit(solution)/shard_map/td,dhe->hte/dot_general | solution.py:117
  366.7 41.0 %convert_bitcast_fusion.1.k_ref = bf16[64,256,128]{2,1,0:T(8,128)(2,1)} fusion(bf16[4096,64,128]{2,1,0:T(8,128)(2,1)} %bitcast.13, bf16[256,4096]{1,0:T(8,128)(2,1)} %copy-done.1, f32[256]{0:T(256)S(1)} %add_rsqrt_fusion, f32[4096]{0:T(1024)S(1)} %bitcast.65), kind=kOutput, calls=%fused_computation.32 | convolution fusion | flops 17186160640 | bytes 73417728 | tf_op jit(solution)/shard_map/td,dhe->hte/dot_general | solution.py:117
  407.7 41.1 %convert_bitcast_fusion.2.q_ref = bf16[64,256,128]{2,1,0:T(8,128)(2,1)} fusion(bf16[4096,64,128]{2,1,0:T(8,128)(2,1)} %bitcast.11, bf16[256,4096]{1,0:T(8,128)(2,1)} %copy-done.1, f32[256]{0:T(256)S(1)} %add_rsqrt_fusion, f32[4096]{0:T(1024)S(1)} %bitcast.66), kind=kOutput, calls=%fused_computation.33 | convolution fusion | flops 17186160640 | bytes 73417728 | tf_op jit(solution)/shard_map/td,dhe->hte/dot_general | solution.py:117
  448.8 44.2 %shard_map.105 = bf16[256,8192]{1,0:T(8,128)(2,1)} custom-call(bf16[64,256,128]{2,1,0:T(8,128)(2,1)} %convert_bitcast_fusion.2.q_ref, bf16[64,256,128]{2,1,0:T(8,128)(2,1)} %convert_bitcast_fusion.1.k_ref, bf16[64,256,128]{2,1,0:T(8,128)(2,1)} %convert_bitcast_fusion.v_ref), custom_call_target="tpu_custom_call" | custom-call | flops 4294967296 | bytes 16777216 | tf_op jit(solution)/shard_map/pallas_call | solution.py:101
  493.1 0.0 copy-start
  493.1 0.0 copy-start.2
  493.1 29.1 %fusion.15 = bf16[256,4096]{1,0:T(8,128)(2,1)} fusion(bf16[256,8192]{1,0:T(8,128)(2,1)} %shard_map.102, bf16[8192,4096]{1,0:T(8,128)(2,1)} %bitcast.17, bf16[256,4096]{1,0:T(8,128)(2,1)S(1)} %collective-permute-done.2), kind=kOutput, calls=%fused_computation.23 | convolution fusion | flops 17185112064 | bytes 75497472 | tf_op jit(solution)/shard_map/dot_general | solution.py:120
  522.2 0.0 copy-done
  522.2 0.0 copy-done.2
  522.2 0.0 copy-start.3
  522.2 27.7 %fusion.13 = bf16[256,4096]{1,0:T(8,128)(2,1)} fusion(bf16[256,8192]{1,0:T(8,128)(2,1)S(1)} %copy-done, bf16[8192,4096]{1,0:T(8,128)(2,1)} %bitcast.17, bf16[256,4096]{1,0:T(8,128)(2,1)S(1)} %copy-done.2), kind=kOutput, calls=%fused_computation.20 | convolution fusion | flops 17185112064 | bytes 75497472 | tf_op jit(solution)/shard_map/dot_general | solution.py:120
  549.9 0.0 copy-done.3
  549.9 4.0 pad_maximum_fusion
  (7 shorter events, 0.0 us)
Async XLA Ops:
  1.5 1.7 collective-permute-start
  20.8 25.9 %collective-permute-start.1 = (f32[256,4096]{1,0:T(8,128)}, f32[256,4096]{1,0:T(8,128)}, u32[]{:S(2)}, u32[]{:S(2)}) collective-permute-start(f32[256,4096]{1,0:T(8,128)} %shard_map.100), channel_id=1, source_target_pairs={{0,1},{1,0},{2,3},{3,2},{4,5},{5,4},{6,7},{7,6}} | collective-permute-start | bytes 12582920 | tf_op jit(solution)/shard_map/ppermute | solution.py:148
  22.7 16.9 %copy-start.4 = (f32[2,2,128,8]{2,3,1,0:T(8,128)S(1)}, f32[2,2,128,8]{2,3,1,0:T(8,128)}, u32[]{:S(2)}) copy-start(f32[2,2,128,8]{2,3,1,0:T(8,128)} %param.13) | copy-start | bytes 49156
  38.7 27.3 %collective-permute-start.3 = (f32[256,4096]{1,0:T(8,128)}, f32[256,4096]{1,0:T(8,128)}, u32[]{:S(2)}, u32[]{:S(2)}) collective-permute-start(f32[256,4096]{1,0:T(8,128)} %shard_map.103), channel_id=1, source_target_pairs={{0,1},{1,0},{2,3},{3,2},{4,5},{5,4},{6,7},{7,6}} | collective-permute-start | bytes 12582920 | tf_op jit(solution)/shard_map/ppermute | solution.py:148
  63.1 50.5 %collective-permute-start.2 = (bf16[256,4096]{1,0:T(8,128)(2,1)}, bf16[256,4096]{1,0:T(8,128)(2,1)S(1)}, u32[]{:S(2)}, u32[]{:S(2)}) collective-permute-start(bf16[256,4096]{1,0:T(8,128)(2,1)} %shard_map.101), channel_id=1, source_target_pairs={{0,2},{2,4},{4,6},{6,0},{1,3},{3,5},{5,7},{7,1}} | collective-permute-start | bytes 6291464 | tf_op jit(solution)/shard_map/ppermute | solution.py:150
  82.4 77.5 %copy-start.5 = (f32[1,4096]{1,0:T(1,128)S(1)}, f32[1,4096]{1,0:T(1,128)}, u32[]{:S(2)}) copy-start(f32[1,4096]{1,0:T(1,128)} %param.15) | copy-start | bytes 49156
  82.4 75.6 %collective-permute-start.4 = (bf16[256,4096]{1,0:T(8,128)(2,1)}, bf16[256,4096]{1,0:T(8,128)(2,1)S(1)}, u32[]{:S(2)}, u32[]{:S(2)}) collective-permute-start(bf16[256,4096]{1,0:T(8,128)(2,1)} %shard_map.104), channel_id=1, source_target_pairs={{0,2},{2,4},{4,6},{6,0},{1,3},{3,5},{5,7},{7,1}} | collective-permute-start | bytes 6291464 | tf_op jit(solution)/shard_map/ppermute | solution.py:150
  158.0 1.3 copy-start.1
  493.1 29.1 %copy-start = (bf16[256,8192]{1,0:T(8,128)(2,1)S(1)}, bf16[256,8192]{1,0:T(8,128)(2,1)}, u32[]{:S(2)}) copy-start(bf16[256,8192]{1,0:T(8,128)(2,1)} %shard_map.105) | copy-start | bytes 12582916
  493.1 29.1 %copy-start.2 = (bf16[256,4096]{1,0:T(8,128)(2,1)S(1)}, bf16[256,4096]{1,0:T(8,128)(2,1)}, u32[]{:S(2)}) copy-start(bf16[256,4096]{1,0:T(8,128)(2,1)} %copy-done.1) | copy-start | bytes 6291460
  522.2 27.7 %copy-start.3 = (bf16[256,4096]{1,0:T(8,128)(2,1)S(1)}, bf16[256,4096]{1,0:T(8,128)(2,1)}, u32[]{:S(2)}) copy-start(bf16[256,4096]{1,0:T(8,128)(2,1)} %fusion.15) | copy-start | bytes 6291460

commit v2 on v0

v2 whole, which is shorter than its diff:
```python
import functools

import jax
import jax.numpy as jnp
from jax import lax
from jax.experimental import pallas as pl
from jax.experimental.pallas import tpu as pltpu
from jax.sharding import PartitionSpec as P


NORM_EPS = 1e-6
GROUP = 8
HALVES = 2


def gates_kernel(code_ref, gate_ref, after_ref, w_ref):
    tokens, top_k = code_ref.shape[1:]
    slots = w_ref.shape[2]
    rows, lanes = 64, 512
    for t0 in range(0, tokens, rows):
        code = code_ref[0, t0:t0 + rows, :]
        gate = gate_ref[0, t0:t0 + rows, :]
        for s0 in range(0, slots, lanes):
            lane = lax.broadcasted_iota(jnp.int32, (rows, lanes), 1) + s0
            full = jnp.zeros((rows, lanes), jnp.float32)
            for i in range(top_k):
                full = jnp.where(lane == code[:, i:i + 1], gate[:, i:i + 1], full)
            for part in range(3):
                val = full.astype(jnp.bfloat16)
                w_ref[0, part * tokens + t0:part * tokens + t0 + rows, s0:s0 + lanes] = val
                full = full - val.astype(jnp.float32)


def gates(code, gate, slots, after):
    rows, tokens, top_k = code.shape
    spec = pl.BlockSpec((1, tokens, top_k), lambda m: (m, 0, 0))
    return pl.pallas_call(
        gates_kernel,
        out_shape=jax.ShapeDtypeStruct((rows, 3 * tokens, slots), jnp.bfloat16),
        grid=(rows,),
        in_specs=[spec, spec, pl.BlockSpec(memory_space=pl.ANY)],
        out_specs=pl.BlockSpec((1, 3 * tokens, slots), lambda m: (m, 0, 0)),
        cost_estimate=pl.CostEstimate(flops=rows * tokens * slots * 64, bytes_accessed=6 * rows * tokens * slots, transcendentals=0),
        name='gates',
    )(code, gate, after)


def mix_kernel(has_add, side_ref, w_ref, exp_ref, after_ref, *rest):
    out_ref = rest[2] if has_add else rest[0]
    slots = w_ref.shape[2]
    tokens = w_ref.shape[1] // 3
    exp_rows = exp_ref[0].reshape(slots, exp_ref.shape[3])
    parts = jnp.dot(w_ref[0], exp_rows, preferred_element_type=jnp.float32)
    total = parts[:tokens] + parts[tokens:2 * tokens] + parts[2 * tokens:]
    if has_add:
        total = total + rest[1][...] + rest[0][...].astype(jnp.float32)
    out_ref[...] = total.astype(out_ref.dtype)
    if has_add:
        square_ref = rest[3]

        @pl.when(pl.program_id(0) == 0)
        def clear():
            square_ref[...] = jnp.zeros_like(square_ref)

        wide = total.astype(jnp.bfloat16).astype(jnp.float32)
        square_ref[...] += jnp.sum(wide * wide, axis=1, keepdims=True)


def mix(expert_out, row, piece, side, w, after, add=None):
    _, rows3, slots = w.shape
    tokens = rows3 // 3
    _, experts, cap, d_model = expert_out.shape
    width = d_model // HALVES
    col = 512
    steps = width // col
    in_specs = [
        pl.BlockSpec((1, rows3, slots), lambda c, s: (row, 0, 0)),
        pl.BlockSpec((1, experts, cap // 2, col), lambda c, s: (row, 0, s[0], piece * steps + c)),
        pl.BlockSpec(memory_space=pl.ANY),
    ]
    args = [w, expert_out, after]
    if add is not None:
        in_specs += [
            pl.BlockSpec((tokens, col), lambda c, s: (row, piece * steps + c)),
            pl.BlockSpec((tokens, col), lambda c, s: (0, c)),
        ]
        args += list(add)
    out_shape = [jax.ShapeDtypeStruct((tokens, width), jnp.float32 if add is None else jnp.bfloat16)]
    out_specs = [pl.BlockSpec((tokens, col), lambda c, s: (0, c))]
    if add is not None:
        out_shape.append(jax.ShapeDtypeStruct((tokens, 128), jnp.float32))
        out_specs.append(pl.BlockSpec((tokens, 128), lambda c, s: (0, 0)))
    return pl.pallas_call(
        functools.partial(mix_kernel, add is not None),
        out_shape=out_shape,
        grid_spec=pltpu.PrefetchScalarGridSpec(
            num_scalar_prefetch=1,
            grid=(steps,),
            in_specs=in_specs,
            out_specs=out_specs,
        ),
        cost_estimate=pl.CostEstimate(flops=2 * rows3 * slots * width, bytes_accessed=2 * slots * width, transcendentals=0),
    )(side.reshape(1), *args)


def normed(y_refs, inv_ref, norm_ref, xs):
    step = pl.program_id(1)

    @pl.when(pl.program_id(0) == 0)
    def make():
        rows = y_refs[0].shape[0]
        for m, y_ref in enumerate(y_refs):
            for t0 in range(0, rows, 64):
                span = slice(m * rows + t0, m * rows + t0 + 64)
                wide = y_ref[t0:t0 + 64, :].astype(jnp.float32)
                xs[step, span, :] = (wide * inv_ref[span, :1] * norm_ref[...]).astype(jnp.bfloat16)

    return xs[step]


def first_kernel(y0_ref, y1_ref, inv_ref, norm_ref, *refs):
    step = pl.program_id(1)
    x = normed((y0_ref, y1_ref), inv_ref, norm_ref, refs[6])
    for w_ref, o_ref in zip(refs[:3], refs[3:6]):
        depth = w_ref.shape[0]
        out = jnp.dot(x, w_ref[...].reshape(depth, -1), preferred_element_type=jnp.float32)

        @pl.when(step == 0)
        def start(out=out, o_ref=o_ref):
            o_ref[...] = out

        @pl.when(step > 0)
        def add(out=out, o_ref=o_ref):
            o_ref[...] += out


def attend(causal, scale, q, k, v):
    dims = (((1,), (1,)), ((), ()))
    scores = [lax.dot_general(a, b, dims, preferred_element_type=jnp.float32) for a, b in zip(q, k)]
    scores = [jnp.where(causal, s * scale, -jnp.inf) for s in scores]
    tops = [jnp.max(s, axis=1, keepdims=True) for s in scores]
    expd = [jnp.exp(s - t) for s, t in zip(scores, tops)]
    inv = [1.0 / jnp.sum(e, axis=1, keepdims=True) for e in expd]
    probs = [(e * i).astype(jnp.bfloat16) for e, i in zip(expd, inv)]
    return [jnp.dot(p, c, preferred_element_type=jnp.float32).astype(jnp.bfloat16) for p, c in zip(probs, v)]


def second_kernel(seq_len, head_dim, y0_ref, y1_ref, inv_ref, norm_ref, *refs):
    w_refs, p_refs, a_ref, accs, qkv = refs[:3], refs[3:6], refs[6], refs[7:10], refs[10]
    step = pl.program_id(1)
    last = pl.num_programs(1) - 1
    x = normed((y0_ref, y1_ref), inv_ref, norm_ref, refs[11])
    for i, w_ref in enumerate(w_refs):
        depth = w_ref.shape[0]
        out = jnp.dot(x, w_ref[...].reshape(depth, -1), preferred_element_type=jnp.float32)

        @pl.when(step == 0)
        def start(i=i, out=out):
            accs[i][...] = p_refs[i][...] + out

        @pl.when(step == last)
        def finish(i=i, out=out):
            qkv[i] = (accs[i][...] + out).astype(jnp.bfloat16)

    @pl.when(step == last)
    def heads():
        tokens, width = a_ref.shape
        row = lax.broadcasted_iota(jnp.int32, (seq_len, seq_len), 0)
        col = lax.broadcasted_iota(jnp.int32, (seq_len, seq_len), 1)
        causal = row >= col
        spans = [(t, h) for h in range(0, width, head_dim) for t in range(0, tokens, seq_len)]
        for n in range(0, len(spans), 8):
            part = spans[n:n + 8]
            args = [[qkv[i, t:t + seq_len, h:h + head_dim] for t, h in part] for i in range(3)]
            for (t, h), out in zip(part, attend(causal, head_dim ** -0.5, *args)):
                a_ref[t:t + seq_len, h:h + head_dim] = out


def project(piece, ys, inv, norm_w, weights, parts, seq_len):
    rows, width = ys[0].shape
    tokens = inv.shape[0]
    _, heads, head_dim = weights[0].shape
    depth = 1024
    steps = width // depth
    cols = GROUP * head_dim
    y_spec = pl.BlockSpec((rows, depth), lambda g, k: (0, jnp.where(g == 0, k, steps - 1)))
    w_spec = pl.BlockSpec((depth, GROUP, head_dim), lambda g, k: (piece * steps + k, g, 0))
    o_spec = pl.BlockSpec((tokens, cols), lambda g, k: (0, g))
    in_specs = [
        y_spec,
        y_spec,
        pl.BlockSpec(inv.shape, lambda g, k: (0, 0)),
        pl.BlockSpec((1, depth), lambda g, k: (0, piece * steps + k)),
    ] + [w_spec] * 3
    xs = pltpu.VMEM((steps, tokens, depth), jnp.bfloat16)
    flops = 6 * tokens * width * heads * head_dim
    settings = dict(
        grid=(heads // GROUP, steps),
        compiler_params=pltpu.CompilerParams(vmem_limit_bytes=56 * 2 ** 20),
        cost_estimate=pl.CostEstimate(flops=flops, bytes_accessed=flops // tokens, transcendentals=0),
    )
    args = (*ys, inv, norm_w, *weights)
    if parts is None:
        return pl.pallas_call(
            first_kernel,
            out_shape=[jax.ShapeDtypeStruct((tokens, heads * head_dim), jnp.float32)] * 3,
            in_specs=in_specs,
            out_specs=[o_spec] * 3,
            scratch_shapes=[xs],
            name='first',
            **settings,
        )(*args)
    assert steps == 2
    return pl.pallas_call(
        functools.partial(second_kernel, seq_len, head_dim),
        out_shape=jax.ShapeDtypeStruct((tokens, heads * head_dim), jnp.bfloat16),
        in_specs=in_specs + [o_spec] * 3,
        out_specs=o_spec,
        scratch_shapes=[pltpu.VMEM((tokens, cols), jnp.float32)] * 3 + [pltpu.VMEM((3, tokens, cols), jnp.bfloat16), xs],
        name='second',
        **settings,
    )(*args, *parts)


def out_kernel(y_refs_per_half, a_ref, w_ref, *refs):
    o_ref = refs[-1]
    out = jnp.dot(a_ref[...], w_ref[...], preferred_element_type=jnp.float32).astype(jnp.bfloat16).astype(jnp.float32)
    steps = pl.num_programs(0) // HALVES
    rows = refs[0].shape[0]
    for c in range(HALVES):

        @pl.when(pl.program_id(0) // steps == c)
        def store(c=c):
            for m in range(y_refs_per_half):
                wide = refs[c * y_refs_per_half + m][...].astype(jnp.float32)
                span = slice(m * rows, (m + 1) * rows)
                o_ref[span, :] = (wide + out[span]).astype(jnp.bfloat16)


def project_out(attn, w_out, ys):
    tokens, inner = attn.shape
    d_model = w_out.shape[1]
    col = 512
    steps = d_model // HALVES // col
    y_specs = [
        pl.BlockSpec((y.shape[0], col), lambda n, c=c: (0, jnp.clip(n - c * steps, 0, steps - 1)))
        for c in range(HALVES) for y in ys[c]
    ]
    flops = 2 * tokens * inner * d_model
    return pl.pallas_call(
        functools.partial(out_kernel, len(ys[0])),
        out_shape=jax.ShapeDtypeStruct((tokens, d_model), jnp.bfloat16),
        grid=(HALVES * steps,),
        in_specs=[pl.BlockSpec((tokens, inner), lambda n: (0, 0)), pl.BlockSpec((inner, col), lambda n: (0, n))] + y_specs,
        out_specs=pl.BlockSpec((tokens, col), lambda n: (0, n)),
        compiler_params=pltpu.CompilerParams(vmem_limit_bytes=56 * 2 ** 20),
        cost_estimate=pl.CostEstimate(flops=flops, bytes_accessed=flops // tokens, transcendentals=0),
        name='out',
    )(attn, w_out, *ys[0], *ys[1])


def solution(mesh):
    stages = mesh.shape['pp']
    send_next = [(src_row, (src_row + 1) % stages) for src_row in range(stages)]
    swap = [(0, 1), (1, 0)]
    tok_spec = P('pp', 'ep', None, None)
    wt_spec = P('pp', None, None, None)

    def step(expert_out, expert_ids, slot_ids, gate_vals, residual, norm_w, w_query, w_key, w_value, w_out):
        num_micro, seqs_dev, seq_len, d_model = residual.shape
        experts, cap = expert_out.shape[1:3]
        half = cap // 2
        slots = experts * half
        tokens = seqs_dev * seq_len
        me = lax.axis_index('ep').astype(jnp.int32)
        code = jnp.where(slot_ids >= 0, expert_ids * half + slot_ids - me * half, -1)
        theirs = lax.ppermute(jnp.stack([code.astype(jnp.float32), gate_vals]), 'ep', swap)
        flat = (num_micro, tokens, -1)
        first = me * slots
        w_own = gates(code.reshape(flat) - first, gate_vals.reshape(flat), slots, norm_w)
        w_their = gates(theirs[0].astype(jnp.int32).reshape(flat) - first, theirs[1].reshape(flat), slots, w_own)
        flat_h = residual.reshape(num_micro * tokens, d_model)
        arrived, squares, after = [], 0.0, w_their
        for c in range(HALVES):
            got = []
            for m in range(num_micro):
                part, = mix(expert_out, m, c, 1 - me, w_their, after)
                got.append(lax.ppermute(part, 'ep', swap))
                after = part
            ys, sums = [], []
            for m in range(num_micro):
                after, total = mix(expert_out, m, c, me, w_own, after, (flat_h, got[m]))
                sums.append(total[:, 0])
                ys.append(lax.ppermute(after, 'pp', send_next))
            arrived.append(ys)
            squares += jnp.stack(sums)
        squares = lax.ppermute(squares, 'pp', send_next)
        inv_rms = lax.rsqrt(squares.reshape(-1, 1) / d_model + NORM_EPS)
        inv_rms = jnp.broadcast_to(inv_rms, (num_micro * tokens, 128))
        weights = (w_query[0], w_key[0], w_value[0])
        out = None
        for c in range(HALVES):
            out = project(c, arrived[c], inv_rms, norm_w, weights, out, seq_len)
        result = project_out(out, w_out[0].reshape(-1, d_model), arrived)
        return result.reshape(num_micro, seqs_dev, seq_len, d_model)

    return jax.shard_map(step, mesh=mesh, in_specs=(tok_spec, tok_spec, tok_spec, tok_spec, tok_spec, P('pp', None), wt_spec, wt_spec, wt_spec, wt_spec), out_specs=tok_spec, check_vma=False)
```

time: 659 us -> 351 us (0.53)
  Pallas kernels: 0 us -> 307 us
  local copies, waits for them, and re-layouts: 236 us -> 11.1 us
  matrix products: 204 us -> 0 us
  waiting for transfers between devices: 127 us -> 20.6 us
  other arithmetic: 57 us -> 1.48 us
  starting transfers between devices: 27.9 us -> 9.35 us
    pallas_call x0 -> x13, Pallas kernels: none -> 307 us  [the longest x1 96.3 us: project(): pl.pallas_call(functools.partial(second_kernel, seq_len, head_dim), out_s...]
    dot_general x6 -> x0, matrix products: 204 us -> none  [the longest x1 44.8 us: attention_block(): jnp.einsum('crif,ife->cre', attn_out, w_out, preferred_element_type=jnp.f...]
    gather x3 -> x0, local copies, waits for them, and re-layouts: 149 us -> none  [gated_sum(): exp_rows[id_blk, pos_blk]]
    ppermute x1 -> x10, waiting for transfers between devices: 89.7 us -> 20.6 us  [the longest x1 20.5 us: step(): squares = lax.ppermute(squares, 'pp', send_next)]
    all_to_all x1 -> x0, local copies, waits for them, and re-layouts: 43.1 us -> none  [device_step(): returned = lax.all_to_all(expert_out, 'ep', 2, 1, tiled=True)]
    unnamed x13 -> x16, local copies, waits for them, and re-layouts: 43.8 us -> 5.5 us
    all_to_all x1 -> x0, waiting for transfers between devices: 37.1 us -> none  [device_step(): returned = lax.all_to_all(expert_out, 'ep', 2, 1, tiled=True)]
    reduce_sum x2 -> x0, other arithmetic: 33.4 us -> none  [the longest x1 32.6 us: gated_sum(): jnp.sum(weight[..., None] * picked.astype(jnp.float32), axis=3)]
  transfers between devices with their start and end apart: 2 -> 10, of which waited for: 2 -> 1; matrix products, arithmetic and copies ran while one was open for 0% -> 2% of each run, Pallas kernels for 0% -> 38%
where the time goes in v2:
time: 351 us; the launch traced here: 350 us
  Pallas kernels  307 us (87%)
  waiting for transfers between devices  20.6 us (6%)
  local copies, waits for them, and re-layouts  11.1 us (3%)
  starting transfers between devices  9.35 us (3%)
    pallas_call x1, Pallas kernels, project(): pl.pallas_call(functools.partial(second_kernel, seq_len, head_dim), out_s...  96.3 us
    pallas_call x1, Pallas kernels, project(): pl.pallas_call(first_kernel, out_shape=[jax.ShapeDtypeStruct((tokens, hea...  82.3 us
    pallas_call x8, Pallas kernels, mix(): pl.pallas_call(functools.partial(mix_kernel, add is not None), out_shape=...  72.6 us
    pallas_call x1, Pallas kernels, project_out(): pl.pallas_call(functools.partial(out_kernel, len(ys[0])), out_shape=jax.S...  44.3 us
    ppermute x1, waiting for transfers between devices, step(): squares = lax.ppermute(squares, 'pp', send_next)  20.5 us
    pallas_call x2, Pallas kernels, gates(): pl.pallas_call(gates_kernel, out_shape=jax.ShapeDtypeStruct((rows, 3 * to...  11.9 us
  transfers between devices with their start and end apart: 10, of which 1 were waited for; matrix products, arithmetic and copies ran while one was open for 2% of the time, Pallas kernels for 38%

profile of v2, /device:TPU:0, one launch (start us, length us, event | category | flops | bytes accessed | tf_op | source)
XLA Modules:
  0.0 350.1 jit_solution(8609043172805047718)
XLA Ops:
  0.0 0.7 convert_bitcast_fusion
  0.7 0.7 pad_maximum_fusion
  1.5 0.8 collective-permute-start
  2.3 1.6 copy.16
  3.9 0.8 copy.15
  4.7 5.9 %gates.2.after_ref.w_ref = bf16[2,768,1536]{2,1,0:T(8,128)(2,1)} custom-call(s32[2,256,8]{2,1,0:T(8,128)} %bitcast.28, f32[2,256,8]{2,1,0:T(8,128)} %bitcast.27, f32[1,4096]{1,0:T(1,128)} %norm_ref.3), custom_call_target="tpu_custom_call" | custom-call | flops 50331648 | bytes 4718592 | tf_op jit(solution)/shard_map/gates/pallas_call | solution.py:37
  10.6 0.0 collective-permute-done
  10.6 0.8 copy.18
  11.5 0.8 copy.17
  12.3 6.0 %gates.3.w_ref.after_ref = bf16[2,768,1536]{2,1,0:T(8,128)(2,1)} custom-call(s32[2,256,8]{2,1,0:T(8,128)} %bitcast.29, f32[2,256,8]{2,1,0:T(8,128)} %bitcast.26, bf16[2,768,1536]{2,1,0:T(8,128)(2,1)} %gates.2.after_ref.w_ref), custom_call_target="tpu_custom_call" | custom-call | flops 50331648 | bytes 4718592 | tf_op jit(solution)/shard_map/gates/pallas_call | solution.py:37
  18.3 8.8 %shard_map.100.after_ref = f32[256,2048]{1,0:T(8,128)} custom-call(s32[1]{0:T(128)} %bitcast.3.side_ref, bf16[2,768,1536]{2,1,0:T(8,128)(2,1)} %gates.3.w_ref.after_ref, bf16[2,64,48,4096]{3,2,1,0:T(8,128)(2,1)} %exp_ref.15, bf16[2,768,1536]{2,1,0:T(8,128)(2,1)} %gates.3.w_ref.after_ref), custom_call_target="tpu_custom_call" | custom-call | flops 4831838208 | bytes 6291456 | tf_op jit(solution)/shard_map/pallas_call | solution.py:93
  27.1 0.0 collective-permute-start.1
  27.1 8.9 %shard_map.101.after_ref = f32[256,2048]{1,0:T(8,128)} custom-call(s32[1]{0:T(128)} %bitcast.3.side_ref, bf16[2,768,1536]{2,1,0:T(8,128)(2,1)} %gates.3.w_ref.after_ref, bf16[2,64,48,4096]{3,2,1,0:T(8,128)(2,1)} %exp_ref.15, f32[256,2048]{1,0:T(8,128)} %shard_map.100.after_ref), custom_call_target="tpu_custom_call" | custom-call | flops 4831838208 | bytes 6291456 | tf_op jit(solution)/shard_map/pallas_call | solution.py:93
  36.0 0.5 collective-permute-start.2
  36.5 0.0 collective-permute-done.1.rest_1_
  36.5 9.3 %shard_map.102 = (bf16[256,2048]{1,0:T(8,128)(2,1)}, f32[256,128]{1,0:T(8,128)}) custom-call(s32[1]{0:T(128)} %bitcast.side_ref, bf16[2,768,1536]{2,1,0:T(8,128)(2,1)} %gates.2.after_ref.w_ref, bf16[2,64,48,4096]{3,2,1,0:T(8,128)(2,1)} %exp_ref.15, f32[256,2048]{1,0:T(8,128)} %shard_map.101.after_ref, bf16[512,4096]{1,0:T(8,128)(2,1)} %bitcast.22, ...), custom_call_target="tpu_custom_call" | custom-call | flops 4831838208 | bytes 6291456 | tf_op jit(solution)/shard_map/pallas_call | solution.py:93
  45.8 0.0 collective-permute-done.2.rest_1_
  45.8 0.0 copy-start.1
  45.8 1.3 copy-done.1
  47.1 9.3 %shard_map.103 = (bf16[256,2048]{1,0:T(8,128)(2,1)}, f32[256,128]{1,0:T(8,128)}) custom-call(s32[1]{0:T(128)} %bitcast.side_ref, bf16[2,768,1536]{2,1,0:T(8,128)(2,1)} %gates.2.after_ref.w_ref, bf16[2,64,48,4096]{3,2,1,0:T(8,128)(2,1)} %exp_ref.15, bf16[256,2048]{1,0:T(8,128)(2,1)} %get-tuple-element.16.after_ref, bf16[512,4096]{1,0:T(8,128)(2,1)} %bitcast.23, ...), custom_call_target="tpu_custom_call" | custom-call | flops 4831838208 | bytes 6291456 | tf_op jit(solution)/shard_map/pallas_call | solution.py:93
  56.3 8.8 %shard_map.104.after_ref = f32[256,2048]{1,0:T(8,128)} custom-call(s32[1]{0:T(128)} %bitcast.3.side_ref, bf16[2,768,1536]{2,1,0:T(8,128)(2,1)} %gates.3.w_ref.after_ref, bf16[2,64,48,4096]{3,2,1,0:T(8,128)(2,1)} %exp_ref.15, bf16[256,2048]{1,0:T(8,128)(2,1)} %get-tuple-element.17.after_ref), custom_call_target="tpu_custom_call" | custom-call | flops 4831838208 | bytes 6291456 | tf_op jit(solution)/shard_map/pallas_call | solution.py:93
  65.2 0.0 copy-start.2
  65.2 0.0 copy-start.5
  65.2 0.0 copy-start.6
  65.2 0.1 collective-permute-start.3
  65.2 9.0 %shard_map.105.after_ref = f32[256,2048]{1,0:T(8,128)} custom-call(s32[1]{0:T(128)} %bitcast.3.side_ref, bf16[2,768,1536]{2,1,0:T(8,128)(2,1)} %gates.3.w_ref.after_ref, bf16[2,64,48,4096]{3,2,1,0:T(8,128)(2,1)} %exp_ref.15, f32[256,2048]{1,0:T(8,128)} %shard_map.104.after_ref), custom_call_target="tpu_custom_call" | custom-call | flops 4831838208 | bytes 6291456 | tf_op jit(solution)/shard_map/pallas_call | solution.py:93
  74.2 0.4 collective-permute-start.5
  74.6 2.6 collective-permute-start.9
  77.2 0.0 copy-done.2
  77.2 1.5 collective-permute-start.8
  78.7 0.0 copy-done.5
  78.7 0.1 slice_reduce_fusion.3
  78.8 0.0 copy-done.6
  78.8 0.1 slice_reduce_fusion.2
  78.9 0.0 collective-permute-done.3.rest_1_
  78.9 9.3 %shard_map.106 = (bf16[256,2048]{1,0:T(8,128)(2,1)}, f32[256,128]{1,0:T(8,128)}) custom-call(s32[1]{0:T(128)} %bitcast.side_ref, bf16[2,768,1536]{2,1,0:T(8,128)(2,1)} %gates.2.after_ref.w_ref, bf16[2,64,48,4096]{3,2,1,0:T(8,128)(2,1)} %exp_ref.15, f32[256,2048]{1,0:T(8,128)} %shard_map.105.after_ref, bf16[512,4096]{1,0:T(8,128)(2,1)} %bitcast.24, ...), custom_call_target="tpu_custom_call" | custom-call | flops 4831838208 | bytes 6291456 | tf_op jit(solution)/shard_map/pallas_call | solution.py:93
  88.2 1.0 slice_reduce_fusion.1
  89.3 0.0 collective-permute-done.5.rest_1_
  89.3 0.0 copy-start
  89.3 1.3 copy-done
  90.6 9.3 %shard_map.107 = (bf16[256,2048]{1,0:T(8,128)(2,1)}, f32[256,128]{1,0:T(8,128)}) custom-call(s32[1]{0:T(128)} %bitcast.side_ref, bf16[2,768,1536]{2,1,0:T(8,128)(2,1)} %gates.2.after_ref.w_ref, bf16[2,64,48,4096]{3,2,1,0:T(8,128)(2,1)} %exp_ref.15, bf16[256,2048]{1,0:T(8,128)(2,1)} %get-tuple-element.18.after_ref, bf16[512,4096]{1,0:T(8,128)(2,1)} %bitcast.25, ...), custom_call_target="tpu_custom_call" | custom-call | flops 4831838208 | bytes 6291456 | tf_op jit(solution)/shard_map/pallas_call | solution.py:93
  99.9 1.0 slice_reduce_fusion
  100.9 1.5 collective-permute-start.7
  102.5 0.0 collective-permute-start.4
  102.5 1.9 collective-permute-start.6
  104.4 20.5 %collective-permute-done.7 = f32[2,256]{1,0:T(2,128)S(1)} collective-permute-done((f32[2,256]{1,0:T(2,128)S(1)}, f32[2,256]{1,0:T(2,128)S(1)}, u32[]{:S(2)}, u32[]{:S(2)}) %collective-permute-start.7) | collective-permute-done | bytes 2080 | tf_op jit(solution)/shard_map/ppermute | solution.py:297
  125.0 0.0 collective-permute-done.9.y1_ref.refs_1_
  125.0 0.0 collective-permute-done.8.y0_ref.refs_0_
  125.0 0.8 broadcast_in_dim.10.inv_ref
  125.8 82.3 %first.1 = (f32[512,8192]{1,0:T(8,128)}, f32[512,8192]{1,0:T(8,128)}, f32[512,8192]{1,0:T(8,128)}) custom-call(bf16[256,2048]{1,0:T(8,128)(2,1)} %collective-permute-done.8.y0_ref.refs_0_, bf16[256,2048]{1,0:T(8,128)(2,1)} %collective-permute-done.9.y1_ref.refs_1_, f32[512,128]{1,0:T(8,128)} %broadcast_in_dim.10.inv_ref, f32[1,4096]{1,0:T(1,128)} %norm_ref.3, ...), custom_call_target="tpu_custom_call" | custom-call | flops 51539607552 | bytes 100663296 | tf_op jit(solution)/shard_map/first/pallas_call | solution.py:204
  208.1 0.0 collective-permute-done.6.y1_ref.refs_3_
  208.1 0.0 copy-start.4
  208.1 0.0 collective-permute-done.4.y0_ref.refs_2_
  208.2 0.0 copy-start.3
  208.2 0.9 copy-done.4
  209.1 0.4 copy-done.3
  209.5 96.3 %second.1.a_ref = bf16[512,8192]{1,0:T(8,128)(2,1)} custom-call(bf16[256,2048]{1,0:T(8,128)(2,1)} %copy-done.3, bf16[256,2048]{1,0:T(8,128)(2,1)} %copy-done.4, f32[512,128]{1,0:T(8,128)} %broadcast_in_dim.10.inv_ref, f32[1,4096]{1,0:T(1,128)} %norm_ref.3, bf16[4096,64,128]{2,1,0:T(8,128)(2,1)} %bitcast.9.refs_0_, bf16[4096,64,128]{2,1,0:T(8,128)(2,1)} %bitcast.10.refs_1_, ...), custom_call_target="tpu_custom_call" | custom-call | flops 51539607552 | bytes 100663296 | tf_op jit(solution)/shard_map/second/pallas_call | solution.py:214
  305.8 44.3 %out.1 = bf16[512,4096]{1,0:T(8,128)(2,1)} custom-call(bf16[512,8192]{1,0:T(8,128)(2,1)} %second.1.a_ref, bf16[8192,4096]{1,0:T(8,128)(2,1)} %bitcast.12.w_ref, bf16[256,2048]{1,0:T(8,128)(2,1)} %collective-permute-done.8.y0_ref.refs_0_, bf16[256,2048]{1,0:T(8,128)(2,1)} %collective-permute-done.9.y1_ref.refs_1_, bf16[256,2048]{1,0:T(8,128)(2,1)} %copy-done.3, ...), custom_call_target="tpu_custom_call" | custom-call | flops 34359738368 | bytes 67108864 | tf_op jit(solution)/shard_map/out/pallas_call | solution.py:250
  (5 shorter events, 0.0 us)
Async XLA Ops:
  1.5 9.2 %collective-permute-start = (f32[2,2,2,128,8]{3,4,2,1,0:T(8,128)S(1)}, f32[2,2,2,128,8]{3,4,2,1,0:T(8,128)S(1)}, u32[]{:S(2)}, u32[]{:S(2)}) collective-permute-start(f32[2,2,2,128,8]{3,4,2,1,0:T(8,128)S(1)} %pad_maximum_fusion), channel_id=1, source_target_pairs={{0,1},{1,0},{2,3},{3,2},{4,5},{5,4},{6,7},{7,6}} | collective-permute-start | bytes 98312 | tf_op jit(solution)/shard_map/ppermute | solution.py:277
  27.1 9.4 %collective-permute-start.1 = (f32[256,2048]{1,0:T(8,128)}, f32[256,2048]{1,0:T(8,128)}, u32[]{:S(2)}, u32[]{:S(2)}) collective-permute-start(f32[256,2048]{1,0:T(8,128)} %shard_map.100.after_ref), channel_id=1, source_target_pairs={{0,1},{1,0},{2,3},{3,2},{4,5},{5,4},{6,7},{7,6}} | collective-permute-start | bytes 6291464 | tf_op jit(solution)/shard_map/ppermute | solution.py:288
  36.0 9.8 %collective-permute-start.2 = (f32[256,2048]{1,0:T(8,128)}, f32[256,2048]{1,0:T(8,128)S(1)}, u32[]{:S(2)}, u32[]{:S(2)}) collective-permute-start(f32[256,2048]{1,0:T(8,128)} %shard_map.101.after_ref), channel_id=1, source_target_pairs={{0,1},{1,0},{2,3},{3,2},{4,5},{5,4},{6,7},{7,6}} | collective-permute-start | bytes 6291464 | tf_op jit(solution)/shard_map/ppermute | solution.py:288
  45.8 1.3 copy-start.1
  65.2 12.0 %copy-start.2 = (bf16[256,2048]{1,0:T(8,128)(2,1)S(1)}, bf16[256,2048]{1,0:T(8,128)(2,1)}, u32[]{:S(2)}) copy-start(bf16[256,2048]{1,0:T(8,128)(2,1)} %get-tuple-element.16.after_ref) | copy-start | bytes 3145732
  65.2 13.5 %copy-start.5 = (f32[256,128]{1,0:T(8,128)S(1)}, f32[256,128]{1,0:T(8,128)}, u32[]{:S(2)}) copy-start(f32[256,128]{1,0:T(8,128)} %get-tuple-element.20) | copy-start | bytes 393220
  65.2 13.6 %copy-start.6 = (f32[256,128]{1,0:T(8,128)S(1)}, f32[256,128]{1,0:T(8,128)}, u32[]{:S(2)}) copy-start(f32[256,128]{1,0:T(8,128)} %get-tuple-element.21) | copy-start | bytes 393220
  65.2 13.7 %collective-permute-start.3 = (f32[256,2048]{1,0:T(8,128)}, f32[256,2048]{1,0:T(8,128)}, u32[]{:S(2)}, u32[]{:S(2)}) collective-permute-start(f32[256,2048]{1,0:T(8,128)} %shard_map.104.after_ref), channel_id=1, source_target_pairs={{0,1},{1,0},{2,3},{3,2},{4,5},{5,4},{6,7},{7,6}} | collective-permute-start | bytes 6291464 | tf_op jit(solution)/shard_map/ppermute | solution.py:288
  74.2 15.1 %collective-permute-start.5 = (f32[256,2048]{1,0:T(8,128)}, f32[256,2048]{1,0:T(8,128)S(1)}, u32[]{:S(2)}, u32[]{:S(2)}) collective-permute-start(f32[256,2048]{1,0:T(8,128)} %shard_map.105.after_ref), channel_id=1, source_target_pairs={{0,1},{1,0},{2,3},{3,2},{4,5},{5,4},{6,7},{7,6}} | collective-permute-start | bytes 6291464 | tf_op jit(solution)/shard_map/ppermute | solution.py:288
  74.6 50.4 %collective-permute-start.9 = (bf16[256,2048]{1,0:T(8,128)(2,1)}, bf16[256,2048]{1,0:T(8,128)(2,1)}, u32[]{:S(2)}, u32[]{:S(2)}) collective-permute-start(bf16[256,2048]{1,0:T(8,128)(2,1)} %get-tuple-element.17.after_ref), channel_id=1, source_target_pairs={{0,2},{2,4},{4,6},{6,0},{1,3},{3,5},{5,7},{7,1}} | collective-permute-start | bytes 3145736 | tf_op jit(solution)/shard_map/ppermute | solution.py:294
  77.2 47.8 %collective-permute-start.8 = (bf16[256,2048]{1,0:T(8,128)(2,1)S(1)}, bf16[256,2048]{1,0:T(8,128)(2,1)}, u32[]{:S(2)}, u32[]{:S(2)}) collective-permute-start(bf16[256,2048]{1,0:T(8,128)(2,1)S(1)} %copy-done.2), channel_id=1, source_target_pairs={{0,2},{2,4},{4,6},{6,0},{1,3},{3,5},{5,7},{7,1}} | collective-permute-start | bytes 3145736 | tf_op jit(solution)/shard_map/ppermute | solution.py:294
  89.3 1.3 copy-start
  100.9 24.0 %collective-permute-start.7 = (f32[2,256]{1,0:T(2,128)S(1)}, f32[2,256]{1,0:T(2,128)S(1)}, u32[]{:S(2)}, u32[]{:S(2)}) collective-permute-start(f32[2,256]{1,0:T(2,128)S(1)} %maximum_add_fusion), channel_id=1, source_target_pairs={{0,2},{2,4},{4,6},{6,0},{1,3},{3,5},{5,7},{7,1}} | collective-permute-start | bytes 6152 | tf_op jit(solution)/shard_map/ppermute | solution.py:297
  102.5 105.7 %collective-permute-start.4 = (bf16[256,2048]{1,0:T(8,128)(2,1)}, bf16[256,2048]{1,0:T(8,128)(2,1)S(1)}, u32[]{:S(2)}, u32[]{:S(2)}) collective-permute-start(bf16[256,2048]{1,0:T(8,128)(2,1)} %get-tuple-element.18.after_ref), channel_id=1, source_target_pairs={{0,2},{2,4},{4,6},{6,0},{1,3},{3,5},{5,7},{7,1}} | collective-permute-start | bytes 3145736 | tf_op jit(solution)/shard_map/ppermute | solution.py:294
  102.5 105.6 %collective-permute-start.6 = (bf16[256,2048]{1,0:T(8,128)(2,1)}, bf16[256,2048]{1,0:T(8,128)(2,1)S(1)}, u32[]{:S(2)}, u32[]{:S(2)}) collective-permute-start(bf16[256,2048]{1,0:T(8,128)(2,1)} %get-tuple-element.19), channel_id=1, source_target_pairs={{0,2},{2,4},{4,6},{6,0},{1,3},{3,5},{5,7},{7,1}} | collective-permute-start | bytes 3145736 | tf_op jit(solution)/shard_map/ppermute | solution.py:294
  208.1 1.0 copy-start.4
  208.2 1.3 copy-start.3

commit v3 on v2

--- a/solution.py
+++ b/solution.py
@@ -9,7 +9,7 @@
 
 
 NORM_EPS = 1e-6
-GROUP = 8
+GROUP = 16
 HALVES = 2
 
 
@@ -40,6 +40,7 @@
         grid=(rows,),
         in_specs=[spec, spec, pl.BlockSpec(memory_space=pl.ANY)],
         out_specs=pl.BlockSpec((1, 3 * tokens, slots), lambda m: (m, 0, 0)),
+        compiler_params=pltpu.CompilerParams(vmem_limit_bytes=16 * 2 ** 20),
         cost_estimate=pl.CostEstimate(flops=rows * tokens * slots * 64, bytes_accessed=6 * rows * tokens * slots, transcendentals=0),
         name='gates',
     )(code, gate, after)
@@ -99,14 +100,13 @@
             in_specs=in_specs,
             out_specs=out_specs,
         ),
+        compiler_params=pltpu.CompilerParams(vmem_limit_bytes=16 * 2 ** 20),
         cost_estimate=pl.CostEstimate(flops=2 * rows3 * slots * width, bytes_accessed=2 * slots * width, transcendentals=0),
     )(side.reshape(1), *args)
 
 
-def normed(y_refs, inv_ref, norm_ref, xs):
-    step = pl.program_id(1)
-
-    @pl.when(pl.program_id(0) == 0)
+def normed(first_step, step, y_refs, inv_ref, norm_ref, xs):
+    @pl.when(first_step)
     def make():
         rows = y_refs[0].shape[0]
         for m, y_ref in enumerate(y_refs):
@@ -120,18 +120,12 @@
 
 def first_kernel(y0_ref, y1_ref, inv_ref, norm_ref, *refs):
     step = pl.program_id(1)
-    x = normed((y0_ref, y1_ref), inv_ref, norm_ref, refs[6])
-    for w_ref, o_ref in zip(refs[:3], refs[3:6]):
+    o_ref = refs[3]
+    x = normed(pl.program_id(0) == 0, step, (y0_ref, y1_ref), inv_ref, norm_ref, refs[4])
+    for i, w_ref in enumerate(refs[:3]):
         depth = w_ref.shape[0]
-        out = jnp.dot(x, w_ref[...].reshape(depth, -1), preferred_element_type=jnp.float32)
-
-        @pl.when(step == 0)
-        def start(out=out, o_ref=o_ref):
-            o_ref[...] = out
-
-        @pl.when(step > 0)
-        def add(out=out, o_ref=o_ref):
-            o_ref[...] += out
+        base = jnp.where(step == 0, 0.0, o_ref[i])
+        o_ref[i] = base + jnp.dot(x, w_ref[...].reshape(depth, -1), preferred_element_type=jnp.float32)
 
 
 def attend(causal, scale, q, k, v):
@@ -146,80 +140,108 @@
 
 
 def second_kernel(seq_len, head_dim, y0_ref, y1_ref, inv_ref, norm_ref, *refs):
-    w_refs, p_refs, a_ref, accs, qkv = refs[:3], refs[3:6], refs[6], refs[7:10], refs[10]
-    step = pl.program_id(1)
-    last = pl.num_programs(1) - 1
-    x = normed((y0_ref, y1_ref), inv_ref, norm_ref, refs[11])
+    w_refs, p_ref, a_ref, acc, qkv, xs = refs[:3], *refs[3:]
+    which, step = pl.program_id(1), pl.program_id(2)
+    last = pl.num_programs(2) - 1
+    x = normed((pl.program_id(0) == 0) & (which == 0), step, (y0_ref, y1_ref), inv_ref, norm_ref, xs)
     for i, w_ref in enumerate(w_refs):
-        depth = w_ref.shape[0]
-        out = jnp.dot(x, w_ref[...].reshape(depth, -1), preferred_element_type=jnp.float32)
-
-        @pl.when(step == 0)
-        def start(i=i, out=out):
-            accs[i][...] = p_refs[i][...] + out
-
-        @pl.when(step == last)
-        def finish(i=i, out=out):
-            qkv[i] = (accs[i][...] + out).astype(jnp.bfloat16)
-
-    @pl.when(step == last)
+
+        @pl.when(which == i)
+        def multiply(i=i, w_ref=w_ref):
+            depth = w_ref.shape[0]
+            base = jnp.where(step == 0, p_ref[0], acc[...])
+            out = base + jnp.dot(x, w_ref[...].reshape(depth, -1), preferred_element_type=jnp.float32)
+            acc[...] = out
+            qkv[i] = out.astype(jnp.bfloat16)
+
+    @pl.when((which == len(w_refs) - 1) & (step == last))
     def heads():
         tokens, width = a_ref.shape
         row = lax.broadcasted_iota(jnp.int32, (seq_len, seq_len), 0)
         col = lax.broadcasted_iota(jnp.int32, (seq_len, seq_len), 1)
         causal = row >= col
-        spans = [(t, h) for h in range(0, width, head_dim) for t in range(0, tokens, seq_len)]
-        for n in range(0, len(spans), 8):
-            part = spans[n:n + 8]
-            args = [[qkv[i, t:t + seq_len, h:h + head_dim] for t, h in part] for i in range(3)]
-            for (t, h), out in zip(part, attend(causal, head_dim ** -0.5, *args)):
-                a_ref[t:t + seq_len, h:h + head_dim] = out
-
-
-def project(piece, ys, inv, norm_w, weights, parts, seq_len):
+        pair = 2 * head_dim
+
+        @pl.loop(0, width // pair)
+        def two_heads(n):
+            cols = pl.ds(pl.multiple_of(n * pair, pair), pair)
+            spans = [(t, h) for h in range(0, pair, head_dim) for t in range(0, tokens, seq_len)]
+            parts = [qkv[i, :, cols] for i in range(3)]
+            args = [[part[t:t + seq_len, h:h + head_dim] for t, h in spans] for part in parts]
+            outs = attend(causal, head_dim ** -0.5, *args)
+            for (t, h), out in zip(spans, outs):
+                a_ref[t:t + seq_len, pl.ds(pl.multiple_of(n * pair + h, head_dim), head_dim)] = out
+
+
+def project_first(ys, inv, norm_w, weights):
+    rows, width = ys[0].shape
+    tokens = inv.shape[0]
+    _, heads, head_dim = weights[0].shape
+    depth = 512
+    steps = width // depth
+    cols = GROUP * head_dim
+    y_spec = pl.BlockSpec((rows, depth), lambda g, k: (0, jnp.where(g == 0, k, steps - 1)))
+    in_specs = [
+        y_spec,
+        y_spec,
+        pl.BlockSpec(inv.shape, lambda g, k: (0, 0)),
+        pl.BlockSpec((1, depth), lambda g, k: (0, k)),
+    ] + [pl.BlockSpec((depth, GROUP, head_dim), lambda g, k: (k, g, 0))] * 3
+    flops = 6 * tokens * width * heads * head_dim
+    return pl.pallas_call(
+        first_kernel,
+        out_shape=jax.ShapeDtypeStruct((3, tokens, heads * head_dim), jnp.float32),
+        grid=(heads // GROUP, steps),
+        in_specs=in_specs,
+        out_specs=pl.BlockSpec((3, tokens, cols), lambda g, k: (0, 0, g)),
+        scratch_shapes=[pltpu.VMEM((steps, tokens, depth), jnp.bfloat16)],
+        compiler_params=pltpu.CompilerParams(vmem_limit_bytes=57 * 2 ** 20),
+        cost_estimate=pl.CostEstimate(flops=flops, bytes_accessed=flops // tokens, transcendentals=0),
+        name='first',
+    )(*ys, inv, norm_w, *weights)
+
+
+def project_second(ys, inv, norm_w, weights, partial, seq_len):
     rows, width = ys[0].shape
     tokens = inv.shape[0]
     _, heads, head_dim = weights[0].shape
     depth = 1024
     steps = width // depth
+    assert steps == 2
     cols = GROUP * head_dim
-    y_spec = pl.BlockSpec((rows, depth), lambda g, k: (0, jnp.where(g == 0, k, steps - 1)))
-    w_spec = pl.BlockSpec((depth, GROUP, head_dim), lambda g, k: (piece * steps + k, g, 0))
-    o_spec = pl.BlockSpec((tokens, cols), lambda g, k: (0, g))
+    y_spec = pl.BlockSpec((rows, depth), lambda g, i, k: (0, jnp.where((g == 0) & (i == 0), k, steps - 1)))
+
+    def w_spec(own):
+        def index(g, i, k):
+            at = jnp.maximum(g * steps + jnp.where(i == own, k, jnp.where(i > own, steps - 1, -1)), 0)
+            return steps + at % steps, at // steps, 0
+
+        return pl.BlockSpec((depth, GROUP, head_dim), index)
+
     in_specs = [
         y_spec,
         y_spec,
-        pl.BlockSpec(inv.shape, lambda g, k: (0, 0)),
-        pl.BlockSpec((1, depth), lambda g, k: (0, piece * steps + k)),
-    ] + [w_spec] * 3
-    xs = pltpu.VMEM((steps, tokens, depth), jnp.bfloat16)
+        pl.BlockSpec(inv.shape, lambda g, i, k: (0, 0)),
+        pl.BlockSpec((1, depth), lambda g, i, k: (0, steps + k)),
+        *(w_spec(own) for own in range(3)),
+        pl.BlockSpec((1, tokens, cols), lambda g, i, k: (i, 0, g)),
+    ]
     flops = 6 * tokens * width * heads * head_dim
-    settings = dict(
-        grid=(heads // GROUP, steps),
-        compiler_params=pltpu.CompilerParams(vmem_limit_bytes=56 * 2 ** 20),
-        cost_estimate=pl.CostEstimate(flops=flops, bytes_accessed=flops // tokens, transcendentals=0),
-    )
-    args = (*ys, inv, norm_w, *weights)
-    if parts is None:
-        return pl.pallas_call(
-            first_kernel,
-            out_shape=[jax.ShapeDtypeStruct((tokens, heads * head_dim), jnp.float32)] * 3,
-            in_specs=in_specs,
-            out_specs=[o_spec] * 3,
-            scratch_shapes=[xs],
-            name='first',
-            **settings,
-        )(*args)
-    assert steps == 2
     return pl.pallas_call(
         functools.partial(second_kernel, seq_len, head_dim),
         out_shape=jax.ShapeDtypeStruct((tokens, heads * head_dim), jnp.bfloat16),
-        in_specs=in_specs + [o_spec] * 3,
-        out_specs=o_spec,
-        scratch_shapes=[pltpu.VMEM((tokens, cols), jnp.float32)] * 3 + [pltpu.VMEM((3, tokens, cols), jnp.bfloat16), xs],
+        grid=(heads // GROUP, 3, steps),
+        in_specs=in_specs,
+        out_specs=pl.BlockSpec((tokens, cols), lambda g, i, k: (0, g)),
+        scratch_shapes=[
+            pltpu.VMEM((tokens, cols), jnp.float32),
+            pltpu.VMEM((3, tokens, cols), jnp.bfloat16),
+            pltpu.VMEM((steps, tokens, depth), jnp.bfloat16),
+        ],
+        compiler_params=pltpu.CompilerParams(vmem_limit_bytes=57 * 2 ** 20),
+        cost_estimate=pl.CostEstimate(flops=flops, bytes_accessed=flops // tokens, transcendentals=0),
         name='second',
-        **settings,
-    )(*args, *parts)
+    )(*ys, inv, norm_w, *weights, partial)
 
 
 def out_kernel(y_refs_per_half, a_ref, w_ref, *refs):
@@ -277,8 +299,7 @@
         theirs = lax.ppermute(jnp.stack([code.astype(jnp.float32), gate_vals]), 'ep', swap)
         flat = (num_micro, tokens, -1)
         first = me * slots
-        w_own = gates(code.reshape(flat) - first, gate_vals.reshape(flat), slots, norm_w)
-        w_their = gates(theirs[0].astype(jnp.int32).reshape(flat) - first, theirs[1].reshape(flat), slots, w_own)
+        w_their = gates(theirs[0].astype(jnp.int32).reshape(flat) - first, theirs[1].reshape(flat), slots, norm_w)
         flat_h = residual.reshape(num_micro * tokens, d_model)
         arrived, squares, after = [], 0.0, w_their
         for c in range(HALVES):
@@ -287,6 +308,8 @@
                 part, = mix(expert_out, m, c, 1 - me, w_their, after)
                 got.append(lax.ppermute(part, 'ep', swap))
                 after = part
+            if c == 0:
+                w_own = gates(code.reshape(flat) - first, gate_vals.reshape(flat), slots, after)
             ys, sums = [], []
             for m in range(num_micro):
                 after, total = mix(expert_out, m, c, me, w_own, after, (flat_h, got[m]))
@@ -298,9 +321,8 @@
         inv_rms = lax.rsqrt(squares.reshape(-1, 1) / d_model + NORM_EPS)
         inv_rms = jnp.broadcast_to(inv_rms, (num_micro * tokens, 128))
         weights = (w_query[0], w_key[0], w_value[0])
-        out = None
-        for c in range(HALVES):
-            out = project(c, arrived[c], inv_rms, norm_w, weights, out, seq_len)
+        partial = project_first(arrived[0], inv_rms, norm_w, weights)
+        out = project_second(arrived[1], inv_rms, norm_w, weights, partial, seq_len)
         result = project_out(out, w_out[0].reshape(-1, d_model), arrived)
         return result.reshape(num_micro, seqs_dev, seq_len, d_model)
 

time: 351 us -> 338 us (0.963)
  Pallas kernels: 307 us -> 293 us
  waiting for transfers between devices: 20.6 us -> 27.3 us
  local copies, waits for them, and re-layouts: 11.1 us -> 4.93 us
    pallas_call x8, Pallas kernels: 72.6 us -> 61.9 us  [mix(): pl.pallas_call(functools.partial(mix_kernel, add is not None), out_shape=...]
    ppermute x1, waiting for transfers between devices: 20.5 us -> 26.4 us  [step(): squares = lax.ppermute(squares, 'pp', send_next)]
    pallas_call x2, Pallas kernels: 11.9 us -> 7.13 us  [gates(): pl.pallas_call(gates_kernel, out_shape=jax.ShapeDtypeStruct((rows, 3 * to...]
  transfers between devices with their start and end apart: 10 -> 10, of which waited for: 1 -> 2; matrix products, arithmetic and copies ran while one was open for 2% -> 1% of each run, Pallas kernels for 38% -> 36%
where the time goes in v3:
time: 338 us; the launch traced here: 337 us
  Pallas kernels  293 us (87%)
  waiting for transfers between devices  27.3 us (8%)
  starting transfers between devices  9.72 us (3%)
  local copies, waits for them, and re-layouts  4.93 us (1%)
    pallas_call x1, Pallas kernels, project_second(): pl.pallas_call(functools.partial(second_kernel, seq_len, head_dim), out_s...  101 us
    pallas_call x1, Pallas kernels, project_first(): pl.pallas_call(first_kernel, out_shape=jax.ShapeDtypeStruct((3, tokens, h...  79 us
    pallas_call x8, Pallas kernels, mix(): pl.pallas_call(functools.partial(mix_kernel, add is not None), out_shape=...  61.9 us
    pallas_call x1, Pallas kernels, project_out(): pl.pallas_call(functools.partial(out_kernel, len(ys[0])), out_shape=jax.S...  44.3 us
    ppermute x1, waiting for transfers between devices, step(): squares = lax.ppermute(squares, 'pp', send_next)  26.4 us
    pallas_call x2, Pallas kernels, gates(): pl.pallas_call(gates_kernel, out_shape=jax.ShapeDtypeStruct((rows, 3 * to...  7.13 us
  transfers between devices with their start and end apart: 10, of which 2 were waited for; matrix products, arithmetic and copies ran while one was open for 1% of the time, Pallas kernels for 36%

profile of v3, /device:TPU:0, one launch (start us, length us, event | category | flops | bytes accessed | tf_op | source)
XLA Modules:
  0.0 336.9 jit_solution(9713051502283182242)
XLA Ops:
  0.0 0.7 convert_bitcast_fusion
  0.7 0.7 pad_maximum_fusion
  1.5 0.8 collective-permute-start
  2.3 0.9 collective-permute-done
  3.2 0.1 copy.18
  3.3 0.1 copy.17
  3.4 0.0 copy-start.2
  3.5 0.7 copy-done.2
  4.2 3.6 %gates.2.w_ref.after_ref = bf16[2,768,1536]{2,1,0:T(8,128)(2,1)S(1)} custom-call(s32[2,256,8]{2,1,0:T(8,128)S(1)} %bitcast.30, f32[2,256,8]{2,1,0:T(8,128)S(1)} %bitcast.28, f32[1,4096]{1,0:T(1,128)S(1)} %copy-done.2), custom_call_target="tpu_custom_call" | custom-call | flops 50331648 | bytes 4718592 | tf_op jit(solution)/shard_map/gates/pallas_call | solution.py:37
  7.7 0.0 copy-start
  7.7 9.3 %shard_map.100.after_ref = f32[256,2048]{1,0:T(8,128)} custom-call(s32[1]{0:T(128)} %bitcast.3.side_ref, bf16[2,768,1536]{2,1,0:T(8,128)(2,1)S(1)} %gates.2.w_ref.after_ref, bf16[2,64,48,4096]{3,2,1,0:T(8,128)(2,1)} %exp_ref.15, bf16[2,768,1536]{2,1,0:T(8,128)(2,1)S(1)} %gates.2.w_ref.after_ref), custom_call_target="tpu_custom_call" | custom-call | flops 4831838208 | bytes 6291456 | tf_op jit(solution)/shard_map/pallas_call | solution.py:94
  17.1 0.0 copy-start.7
  17.1 0.3 collective-permute-start.1
  17.4 0.0 copy-done
  17.4 7.2 %shard_map.101.after_ref = f32[256,2048]{1,0:T(8,128)S(1)} custom-call(s32[1]{0:T(128)} %bitcast.3.side_ref, bf16[2,768,1536]{2,1,0:T(8,128)(2,1)S(1)} %gates.2.w_ref.after_ref, bf16[2,64,48,4096]{3,2,1,0:T(8,128)(2,1)} %exp_ref.15, f32[256,2048]{1,0:T(8,128)} %shard_map.100.after_ref), custom_call_target="tpu_custom_call" | custom-call | flops 4831838208 | bytes 6291456 | tf_op jit(solution)/shard_map/pallas_call | solution.py:94
  24.6 0.2 collective-permute-start.2
  24.8 0.0 copy-done.7
  24.8 0.1 copy.16
  24.9 0.1 copy.15
  25.0 0.0 copy-start.1
  25.0 0.0 slice-start
  25.0 3.6 %gates.3.w_ref = bf16[2,768,1536]{2,1,0:T(8,128)(2,1)S(1)} custom-call(s32[2,256,8]{2,1,0:T(8,128)S(1)} %bitcast.31, f32[2,256,8]{2,1,0:T(8,128)S(1)} %bitcast.29, f32[256,2048]{1,0:T(8,128)S(1)} %shard_map.101.after_ref), custom_call_target="tpu_custom_call" | custom-call | flops 50331648 | bytes 4718592 | tf_op jit(solution)/shard_map/gates/pallas_call | solution.py:37
  28.6 0.0 collective-permute-done.1.rest_1_
  28.6 0.0 copy-done.1
  28.6 0.0 slice-start.1
  28.7 7.8 %shard_map.102 = (bf16[256,2048]{1,0:T(8,128)(2,1)S(1)}, f32[256,128]{1,0:T(8,128)S(1)}) custom-call(s32[1]{0:T(128)} %bitcast.side_ref, bf16[2,768,1536]{2,1,0:T(8,128)(2,1)S(1)} %gates.3.w_ref, bf16[2,64,48,4096]{3,2,1,0:T(8,128)(2,1)} %exp_ref.15, f32[256,2048]{1,0:T(8,128)S(1)} %shard_map.101.after_ref, bf16[512,4096]{1,0:T(8,128)(2,1)S(1)} %bitcast.24, ...), custom_call_target="tpu_custom_call" | custom-call | flops 4831838208 | bytes 6291456 | tf_op jit(solution)/shard_map/pallas_call | solution.py:94
  36.4 0.0 collective-permute-done.2.rest_1_
  36.5 7.7 %shard_map.103 = (bf16[256,2048]{1,0:T(8,128)(2,1)S(1)}, f32[256,128]{1,0:T(8,128)S(1)}) custom-call(s32[1]{0:T(128)} %bitcast.side_ref, bf16[2,768,1536]{2,1,0:T(8,128)(2,1)S(1)} %gates.3.w_ref, bf16[2,64,48,4096]{3,2,1,0:T(8,128)(2,1)} %exp_ref.15, bf16[256,2048]{1,0:T(8,128)(2,1)S(1)} %get-tuple-element.13.after_ref, bf16[512,4096]{1,0:T(8,128)(2,1)S(1)} %bitcast.25, ...), custom_call_target="tpu_custom_call" | custom-call | flops 4831838208 | bytes 6291456 | tf_op jit(solution)/shard_map/pallas_call | solution.py:94
  44.2 0.0 slice-done
  44.2 0.0 slice-done.1
  44.2 7.2 %shard_map.104.after_ref = f32[256,2048]{1,0:T(8,128)S(1)} custom-call(s32[1]{0:T(128)} %bitcast.3.side_ref, bf16[2,768,1536]{2,1,0:T(8,128)(2,1)S(1)} %bitcast.23, bf16[2,64,48,4096]{3,2,1,0:T(8,128)(2,1)} %exp_ref.15, bf16[256,2048]{1,0:T(8,128)(2,1)S(1)} %get-tuple-element.14.after_ref), custom_call_target="tpu_custom_call" | custom-call | flops 4831838208 | bytes 6291456 | tf_op jit(solution)/shard_map/pallas_call | solution.py:94
  51.4 0.4 collective-permute-start.3
  51.9 7.1 %shard_map.105.after_ref = f32[256,2048]{1,0:T(8,128)S(1)} custom-call(s32[1]{0:T(128)} %bitcast.3.side_ref, bf16[2,768,1536]{2,1,0:T(8,128)(2,1)S(1)} %bitcast.23, bf16[2,64,48,4096]{3,2,1,0:T(8,128)(2,1)} %exp_ref.15, f32[256,2048]{1,0:T(8,128)S(1)} %shard_map.104.after_ref), custom_call_target="tpu_custom_call" | custom-call | flops 4831838208 | bytes 6291456 | tf_op jit(solution)/shard_map/pallas_call | solution.py:94
  59.0 0.1 collective-permute-start.5
  59.1 2.8 collective-permute-start.9
  61.9 1.5 collective-permute-start.8
  63.4 0.1 slice_reduce_fusion.3
  63.5 0.1 slice_reduce_fusion.2
  63.7 0.0 collective-permute-done.3.rest_1_
  63.7 7.8 %shard_map.106 = (bf16[256,2048]{1,0:T(8,128)(2,1)S(1)}, f32[256,128]{1,0:T(8,128)S(1)}) custom-call(s32[1]{0:T(128)} %bitcast.side_ref, bf16[2,768,1536]{2,1,0:T(8,128)(2,1)S(1)} %gates.3.w_ref, bf16[2,64,48,4096]{3,2,1,0:T(8,128)(2,1)} %exp_ref.15, f32[256,2048]{1,0:T(8,128)S(1)} %shard_map.105.after_ref, bf16[512,4096]{1,0:T(8,128)(2,1)S(1)} %bitcast.26, ...), custom_call_target="tpu_custom_call" | custom-call | flops 4831838208 | bytes 6291456 | tf_op jit(solution)/shard_map/pallas_call | solution.py:94
  71.4 0.1 slice_reduce_fusion.1
  71.6 0.0 collective-permute-done.5.rest_1_
  71.6 7.8 %shard_map.107 = (bf16[256,2048]{1,0:T(8,128)(2,1)S(1)}, f32[256,128]{1,0:T(8,128)S(1)}) custom-call(s32[1]{0:T(128)} %bitcast.side_ref, bf16[2,768,1536]{2,1,0:T(8,128)(2,1)S(1)} %gates.3.w_ref, bf16[2,64,48,4096]{3,2,1,0:T(8,128)(2,1)} %exp_ref.15, bf16[256,2048]{1,0:T(8,128)(2,1)S(1)} %get-tuple-element.15.after_ref, bf16[512,4096]{1,0:T(8,128)(2,1)S(1)} %bitcast.27, ...), custom_call_target="tpu_custom_call" | custom-call | flops 4831838208 | bytes 6291456 | tf_op jit(solution)/shard_map/pallas_call | solution.py:94
  79.4 0.1 slice_reduce_fusion
  79.5 1.5 collective-permute-start.7
  81.0 0.0 collective-permute-start.4
  81.0 1.9 collective-permute-start.6
  83.0 26.4 %collective-permute-done.7 = f32[2,256]{1,0:T(2,128)S(1)} collective-permute-done((f32[2,256]{1,0:T(2,128)S(1)}, f32[2,256]{1,0:T(2,128)S(1)}, u32[]{:S(2)}, u32[]{:S(2)}) %collective-permute-start.7) | collective-permute-done | bytes 2080 | tf_op jit(solution)/shard_map/ppermute | solution.py:320
  109.4 0.0 collective-permute-done.9.y1_ref.refs_1_
  109.4 0.0 copy-start.3
  109.4 0.0 collective-permute-done.8.y0_ref.refs_0_
  109.4 0.0 copy-start.4
  109.5 1.0 broadcast_in_dim.10.inv_ref
  110.5 0.1 copy-done.3
  110.6 0.3 copy-done.4
  110.8 79.0 %first.1.refs_3_ = f32[3,512,8192]{2,1,0:T(8,128)} custom-call(bf16[256,2048]{1,0:T(8,128)(2,1)} %copy-done.4, bf16[256,2048]{1,0:T(8,128)(2,1)} %copy-done.3, f32[512,128]{1,0:T(8,128)} %broadcast_in_dim.10.inv_ref, f32[1,4096]{1,0:T(1,128)} %norm_ref.3, bf16[4096,64,128]{2,1,0:T(8,128)(2,1)} %bitcast.9.refs_0_, bf16[4096,64,128]{2,1,0:T(8,128)(2,1)} %bitcast.10.refs_1_, ...), custom_call_target="tpu_custom_call" | custom-call | flops 51539607552 | bytes 100663296 | tf_op jit(solution)/shard_map/first/pallas_call | solution.py:191
  189.8 0.0 collective-permute-done.6.y1_ref.refs_3_
  189.8 0.0 copy-start.6
  189.8 0.0 collective-permute-done.4.y0_ref.refs_2_
  189.8 0.9 copy-done.6
  190.8 0.0 copy-start.5
  190.8 1.0 copy-done.5
  191.7 100.9 %second.1.a_ref = bf16[512,8192]{1,0:T(8,128)(2,1)} custom-call(bf16[256,2048]{1,0:T(8,128)(2,1)} %copy-done.5, bf16[256,2048]{1,0:T(8,128)(2,1)} %copy-done.6, f32[512,128]{1,0:T(8,128)} %broadcast_in_dim.10.inv_ref, f32[1,4096]{1,0:T(1,128)} %norm_ref.3, bf16[4096,64,128]{2,1,0:T(8,128)(2,1)} %bitcast.9.refs_0_, bf16[4096,64,128]{2,1,0:T(8,128)(2,1)} %bitcast.10.refs_1_, ...), custom_call_target="tpu_custom_call" | custom-call | flops 51539607552 | bytes 100663296 | tf_op jit(solution)/shard_map/second/pallas_call | solution.py:230
  292.6 44.3 %out.1 = bf16[512,4096]{1,0:T(8,128)(2,1)} custom-call(bf16[512,8192]{1,0:T(8,128)(2,1)} %second.1.a_ref, bf16[8192,4096]{1,0:T(8,128)(2,1)} %bitcast.12.w_ref, bf16[256,2048]{1,0:T(8,128)(2,1)} %copy-done.4, bf16[256,2048]{1,0:T(8,128)(2,1)} %copy-done.3, bf16[256,2048]{1,0:T(8,128)(2,1)} %copy-done.5, bf16[256,2048]{1,0:T(8,128)(2,1)} %copy-done.6), custom_call_target="tpu_custom_call" | custom-call | flops 34359738368 | bytes 67108864 | tf_op jit(solution)/shard_map/out/pallas_call | solution.py:272
  (6 shorter events, 0.0 us)
Async XLA Ops:
  1.5 1.7 collective-permute-start
  3.4 0.7 copy-start.2
  7.7 9.7 %copy-start = (bf16[2,768,1536]{2,1,0:T(8,128)(2,1)}, bf16[2,768,1536]{2,1,0:T(8,128)(2,1)S(1)}, u32[]{:S(2)}) copy-start(bf16[2,768,1536]{2,1,0:T(8,128)(2,1)S(1)} %gates.2.w_ref.after_ref) | copy-start | bytes 14155780
  17.1 7.7 %copy-start.7 = (f32[2,2,128,8]{2,3,1,0:T(8,128)S(1)}, f32[2,2,128,8]{2,3,1,0:T(8,128)}, u32[]{:S(2)}) copy-start(f32[2,2,128,8]{2,3,1,0:T(8,128)} %param.13) | copy-start | bytes 49156
  17.1 11.6 %collective-permute-start.1 = (f32[256,2048]{1,0:T(8,128)}, f32[256,2048]{1,0:T(8,128)}, u32[]{:S(2)}, u32[]{:S(2)}) collective-permute-start(f32[256,2048]{1,0:T(8,128)} %shard_map.100.after_ref), channel_id=1, source_target_pairs={{0,1},{1,0},{2,3},{3,2},{4,5},{5,4},{6,7},{7,6}} | collective-permute-start | bytes 6291464 | tf_op jit(solution)/shard_map/ppermute | solution.py:309
  24.6 11.9 %collective-permute-start.2 = (f32[256,2048]{1,0:T(8,128)S(1)}, f32[256,2048]{1,0:T(8,128)}, u32[]{:S(2)}, u32[]{:S(2)}) collective-permute-start(f32[256,2048]{1,0:T(8,128)S(1)} %shard_map.101.after_ref), channel_id=1, source_target_pairs={{0,1},{1,0},{2,3},{3,2},{4,5},{5,4},{6,7},{7,6}} | collective-permute-start | bytes 6291464 | tf_op jit(solution)/shard_map/ppermute | solution.py:309
  25.0 3.6 %copy-start.1 = (bf16[2,2,128,4096]{3,2,1,0:T(8,128)(2,1)S(1)}, bf16[2,2,128,4096]{3,2,1,0:T(8,128)(2,1)}, u32[]{:S(2)}) copy-start(bf16[2,2,128,4096]{3,2,1,0:T(8,128)(2,1)} %param.14) | copy-start | bytes 12582916
  25.0 19.2 %slice-start = ((s8[4718592]{0:T(1024)(128)(4,1)}), s8[4194304]{0:T(1024)(128)(4,1)S(1)}, s32[]{:S(2)}) async-start(s8[4718592]{0:T(1024)(128)(4,1)} %bitcast.22), calls=%async_computation | async-start | bytes 8388608
  28.6 15.5 %slice-start.1 = ((s8[4718592]{0:T(1024)(128)(4,1)}), s8[524288]{0:T(1024)(128)(4,1)S(1)}, s32[]{:S(2)}) async-start(s8[4718592]{0:T(1024)(128)(4,1)} %bitcast.22), calls=%async_computation.1 | async-start | bytes 1048576
  51.4 12.3 %collective-permute-start.3 = (f32[256,2048]{1,0:T(8,128)S(1)}, f32[256,2048]{1,0:T(8,128)S(1)}, u32[]{:S(2)}, u32[]{:S(2)}) collective-permute-start(f32[256,2048]{1,0:T(8,128)S(1)} %shard_map.104.after_ref), channel_id=1, source_target_pairs={{0,1},{1,0},{2,3},{3,2},{4,5},{5,4},{6,7},{7,6}} | collective-permute-start | bytes 6291464 | tf_op jit(solution)/shard_map/ppermute | solution.py:309
  59.0 12.6 %collective-permute-start.5 = (f32[256,2048]{1,0:T(8,128)S(1)}, f32[256,2048]{1,0:T(8,128)S(1)}, u32[]{:S(2)}, u32[]{:S(2)}) collective-permute-start(f32[256,2048]{1,0:T(8,128)S(1)} %shard_map.105.after_ref), channel_id=1, source_target_pairs={{0,1},{1,0},{2,3},{3,2},{4,5},{5,4},{6,7},{7,6}} | collective-permute-start | bytes 6291464 | tf_op jit(solution)/shard_map/ppermute | solution.py:309
  59.1 50.3 %collective-permute-start.9 = (bf16[256,2048]{1,0:T(8,128)(2,1)S(1)}, bf16[256,2048]{1,0:T(8,128)(2,1)S(1)}, u32[]{:S(2)}, u32[]{:S(2)}) collective-permute-start(bf16[256,2048]{1,0:T(8,128)(2,1)S(1)} %get-tuple-element.14.after_ref), channel_id=1, source_target_pairs={{0,2},{2,4},{4,6},{6,0},{1,3},{3,5},{5,7},{7,1}} | collective-permute-start | bytes 3145736 | tf_op jit(solution)/shard_map/ppermute | solution.py:317
  61.9 47.5 %collective-permute-start.8 = (bf16[256,2048]{1,0:T(8,128)(2,1)S(1)}, bf16[256,2048]{1,0:T(8,128)(2,1)S(1)}, u32[]{:S(2)}, u32[]{:S(2)}) collective-permute-start(bf16[256,2048]{1,0:T(8,128)(2,1)S(1)} %get-tuple-element.13.after_ref), channel_id=1, source_target_pairs={{0,2},{2,4},{4,6},{6,0},{1,3},{3,5},{5,7},{7,1}} | collective-permute-start | bytes 3145736 | tf_op jit(solution)/shard_map/ppermute | solution.py:317
  79.5 29.9 %collective-permute-start.7 = (f32[2,256]{1,0:T(2,128)S(1)}, f32[2,256]{1,0:T(2,128)S(1)}, u32[]{:S(2)}, u32[]{:S(2)}) collective-permute-start(f32[2,256]{1,0:T(2,128)S(1)} %maximum_add_fusion), channel_id=1, source_target_pairs={{0,2},{2,4},{4,6},{6,0},{1,3},{3,5},{5,7},{7,1}} | collective-permute-start | bytes 6152 | tf_op jit(solution)/shard_map/ppermute | solution.py:320
  81.0 108.8 %collective-permute-start.4 = (bf16[256,2048]{1,0:T(8,128)(2,1)S(1)}, bf16[256,2048]{1,0:T(8,128)(2,1)S(1)}, u32[]{:S(2)}, u32[]{:S(2)}) collective-permute-start(bf16[256,2048]{1,0:T(8,128)(2,1)S(1)} %get-tuple-element.15.after_ref), channel_id=1, source_target_pairs={{0,2},{2,4},{4,6},{6,0},{1,3},{3,5},{5,7},{7,1}} | collective-permute-start | bytes 3145736 | tf_op jit(solution)/shard_map/ppermute | solution.py:317
  81.0 108.8 %collective-permute-start.6 = (bf16[256,2048]{1,0:T(8,128)(2,1)S(1)}, bf16[256,2048]{1,0:T(8,128)(2,1)S(1)}, u32[]{:S(2)}, u32[]{:S(2)}) collective-permute-start(bf16[256,2048]{1,0:T(8,128)(2,1)S(1)} %get-tuple-element.16), channel_id=1, source_target_pairs={{0,2},{2,4},{4,6},{6,0},{1,3},{3,5},{5,7},{7,1}} | collective-permute-start | bytes 3145736 | tf_op jit(solution)/shard_map/ppermute | solution.py:317
  109.4 1.1 copy-start.3
  109.4 1.4 copy-start.4
  189.8 0.9 copy-start.6
  190.8 1.0 copy-start.5

commit v4 on v2

--- a/solution.py
+++ b/solution.py
@@ -40,6 +40,7 @@
         grid=(rows,),
         in_specs=[spec, spec, pl.BlockSpec(memory_space=pl.ANY)],
         out_specs=pl.BlockSpec((1, 3 * tokens, slots), lambda m: (m, 0, 0)),
+        compiler_params=pltpu.CompilerParams(vmem_limit_bytes=16 * 2 ** 20),
         cost_estimate=pl.CostEstimate(flops=rows * tokens * slots * 64, bytes_accessed=6 * rows * tokens * slots, transcendentals=0),
         name='gates',
     )(code, gate, after)
@@ -50,7 +51,11 @@
     slots = w_ref.shape[2]
     tokens = w_ref.shape[1] // 3
     exp_rows = exp_ref[0].reshape(slots, exp_ref.shape[3])
-    parts = jnp.dot(w_ref[0], exp_rows, preferred_element_type=jnp.float32)
+    middle = 3 * tokens // 2
+    parts = jnp.concatenate([
+        jnp.dot(w_ref[0, :middle], exp_rows, preferred_element_type=jnp.float32),
+        jnp.dot(w_ref[0, middle:], exp_rows, preferred_element_type=jnp.float32),
+    ])
     total = parts[:tokens] + parts[tokens:2 * tokens] + parts[2 * tokens:]
     if has_add:
         total = total + rest[1][...] + rest[0][...].astype(jnp.float32)
@@ -99,39 +104,38 @@
             in_specs=in_specs,
             out_specs=out_specs,
         ),
+        compiler_params=pltpu.CompilerParams(vmem_limit_bytes=16 * 2 ** 20),
         cost_estimate=pl.CostEstimate(flops=2 * rows3 * slots * width, bytes_accessed=2 * slots * width, transcendentals=0),
     )(side.reshape(1), *args)
 
 
-def normed(y_refs, inv_ref, norm_ref, xs):
-    step = pl.program_id(1)
-
-    @pl.when(pl.program_id(0) == 0)
+def normed(first_step, y_refs, inv_ref, norm_ref, xs):
+    @pl.when(first_step)
     def make():
         rows = y_refs[0].shape[0]
         for m, y_ref in enumerate(y_refs):
-            for t0 in range(0, rows, 64):
-                span = slice(m * rows + t0, m * rows + t0 + 64)
-                wide = y_ref[t0:t0 + 64, :].astype(jnp.float32)
-                xs[step, span, :] = (wide * inv_ref[span, :1] * norm_ref[...]).astype(jnp.bfloat16)
-
-    return xs[step]
+
+            @pl.loop(0, rows // 32)
+            def block(n, m=m, y_ref=y_ref):
+                near = pl.ds(pl.multiple_of(n * 32, 32), 32)
+                span = pl.ds(pl.multiple_of(m * rows + n * 32, 32), 32)
+                wide = y_ref[near, :].astype(jnp.float32)
+                xs[span, :] = (wide * inv_ref[span, :1] * norm_ref[...]).astype(jnp.bfloat16)
+
+
+def matmul(xs, w_ref):
+    return jnp.dot(xs[...], w_ref[...].reshape(w_ref.shape[0], -1), preferred_element_type=jnp.float32)
 
 
 def first_kernel(y0_ref, y1_ref, inv_ref, norm_ref, *refs):
-    step = pl.program_id(1)
-    x = normed((y0_ref, y1_ref), inv_ref, norm_ref, refs[6])
-    for w_ref, o_ref in zip(refs[:3], refs[3:6]):
-        depth = w_ref.shape[0]
-        out = jnp.dot(x, w_ref[...].reshape(depth, -1), preferred_element_type=jnp.float32)
-
-        @pl.when(step == 0)
-        def start(out=out, o_ref=o_ref):
-            o_ref[...] = out
-
-        @pl.when(step > 0)
-        def add(out=out, o_ref=o_ref):
-            o_ref[...] += out
+    which = pl.program_id(1)
+    w_refs, o_ref, xs = refs[:3], *refs[3:]
+    normed((pl.program_id(0) == 0) & (which == 0), (y0_ref, y1_ref), inv_ref, norm_ref, xs)
+    for i, w_ref in enumerate(w_refs):
+
+        @pl.when(which == i)
+        def multiply(w_ref=w_ref):
+            o_ref[0] = matmul(xs, w_ref)
 
 
 def attend(causal, scale, q, k, v):
@@ -146,80 +150,85 @@
 
 
 def second_kernel(seq_len, head_dim, y0_ref, y1_ref, inv_ref, norm_ref, *refs):
-    w_refs, p_refs, a_ref, accs, qkv = refs[:3], refs[3:6], refs[6], refs[7:10], refs[10]
-    step = pl.program_id(1)
-    last = pl.num_programs(1) - 1
-    x = normed((y0_ref, y1_ref), inv_ref, norm_ref, refs[11])
-    for i, w_ref in enumerate(w_refs):
-        depth = w_ref.shape[0]
-        out = jnp.dot(x, w_ref[...].reshape(depth, -1), preferred_element_type=jnp.float32)
-
-        @pl.when(step == 0)
-        def start(i=i, out=out):
-            accs[i][...] = p_refs[i][...] + out
-
-        @pl.when(step == last)
-        def finish(i=i, out=out):
-            qkv[i] = (accs[i][...] + out).astype(jnp.bfloat16)
-
-    @pl.when(step == last)
-    def heads():
-        tokens, width = a_ref.shape
+    w_refs, p_ref, a_ref, qkv, xs = refs[:3], *refs[3:]
+    group, which = pl.program_id(0), pl.program_id(1)
+    groups = pl.num_programs(0) - 1
+    tokens, width = a_ref.shape
+    heads = width // head_dim
+    normed((group == 0) & (which == 0), (y0_ref, y1_ref), inv_ref, norm_ref, xs)
+    now, before = lax.rem(group, 2), lax.rem(group + 1, 2)
+    bounds = [-(-heads * i // 3) for i in range(4)]
+
+    def attend_some(i):
         row = lax.broadcasted_iota(jnp.int32, (seq_len, seq_len), 0)
         col = lax.broadcasted_iota(jnp.int32, (seq_len, seq_len), 1)
-        causal = row >= col
-        spans = [(t, h) for h in range(0, width, head_dim) for t in range(0, tokens, seq_len)]
-        for n in range(0, len(spans), 8):
-            part = spans[n:n + 8]
-            args = [[qkv[i, t:t + seq_len, h:h + head_dim] for t, h in part] for i in range(3)]
-            for (t, h), out in zip(part, attend(causal, head_dim ** -0.5, *args)):
+        for h in range(bounds[i] * head_dim, bounds[i + 1] * head_dim, head_dim):
+            spans = range(0, tokens, seq_len)
+            args = [[qkv[before, j, t:t + seq_len, h:h + head_dim] for t in spans] for j in range(3)]
+            for t, out in zip(spans, attend(row >= col, head_dim ** -0.5, *args)):
                 a_ref[t:t + seq_len, h:h + head_dim] = out
 
-
-def project(piece, ys, inv, norm_w, weights, parts, seq_len):
+    for i, w_ref in enumerate(w_refs):
+
+        @pl.when((which == i) & (group < groups))
+        def both(i=i, w_ref=w_ref):
+            qkv[now, i] = (p_ref[0] + matmul(xs, w_ref)).astype(jnp.bfloat16)
+            attend_some(i)
+
+        @pl.when((which == i) & (group == groups))
+        def rest(i=i):
+            attend_some(i)
+
+
+def project(piece, ys, inv, norm_w, weights, partial, seq_len):
     rows, width = ys[0].shape
     tokens = inv.shape[0]
     _, heads, head_dim = weights[0].shape
-    depth = 1024
-    steps = width // depth
     cols = GROUP * head_dim
-    y_spec = pl.BlockSpec((rows, depth), lambda g, k: (0, jnp.where(g == 0, k, steps - 1)))
-    w_spec = pl.BlockSpec((depth, GROUP, head_dim), lambda g, k: (piece * steps + k, g, 0))
-    o_spec = pl.BlockSpec((tokens, cols), lambda g, k: (0, g))
+    groups = heads // GROUP
+
+    def w_spec(own):
+        def index(g, i):
+            return piece, jnp.clip(jnp.where(i >= own, g, g - 1), 0, groups - 1), 0
+
+        return pl.BlockSpec((width, GROUP, head_dim), index)
+
+    whole = pl.BlockSpec((rows, width), lambda g, i: (0, 0))
     in_specs = [
-        y_spec,
-        y_spec,
-        pl.BlockSpec(inv.shape, lambda g, k: (0, 0)),
-        pl.BlockSpec((1, depth), lambda g, k: (0, piece * steps + k)),
-    ] + [w_spec] * 3
-    xs = pltpu.VMEM((steps, tokens, depth), jnp.bfloat16)
+        whole,
+        whole,
+        pl.BlockSpec(inv.shape, lambda g, i: (0, 0)),
+        pl.BlockSpec((1, width), lambda g, i: (0, piece)),
+        *(w_spec(own) for own in range(3)),
+    ]
+    xs = pltpu.VMEM((tokens, width), jnp.bfloat16)
     flops = 6 * tokens * width * heads * head_dim
     settings = dict(
-        grid=(heads // GROUP, steps),
-        compiler_params=pltpu.CompilerParams(vmem_limit_bytes=56 * 2 ** 20),
+        compiler_params=pltpu.CompilerParams(vmem_limit_bytes=57 * 2 ** 20),
         cost_estimate=pl.CostEstimate(flops=flops, bytes_accessed=flops // tokens, transcendentals=0),
     )
     args = (*ys, inv, norm_w, *weights)
-    if parts is None:
+    if partial is None:
         return pl.pallas_call(
             first_kernel,
-            out_shape=[jax.ShapeDtypeStruct((tokens, heads * head_dim), jnp.float32)] * 3,
+            out_shape=jax.ShapeDtypeStruct((3, tokens, heads * head_dim), jnp.float32),
+            grid=(groups, 3),
             in_specs=in_specs,
-            out_specs=[o_spec] * 3,
+            out_specs=pl.BlockSpec((1, tokens, cols), lambda g, i: (i, 0, g)),
             scratch_shapes=[xs],
             name='first',
             **settings,
         )(*args)
-    assert steps == 2
     return pl.pallas_call(
         functools.partial(second_kernel, seq_len, head_dim),
         out_shape=jax.ShapeDtypeStruct((tokens, heads * head_dim), jnp.bfloat16),
-        in_specs=in_specs + [o_spec] * 3,
-        out_specs=o_spec,
-        scratch_shapes=[pltpu.VMEM((tokens, cols), jnp.float32)] * 3 + [pltpu.VMEM((3, tokens, cols), jnp.bfloat16), xs],
+        grid=(groups + 1, 3),
+        in_specs=in_specs + [pl.BlockSpec((1, tokens, cols), lambda g, i: (jnp.where(g < groups, i, 2), 0, jnp.minimum(g, groups - 1)))],
+        out_specs=pl.BlockSpec((tokens, cols), lambda g, i: (0, jnp.maximum(g - 1, 0))),
+        scratch_shapes=[pltpu.VMEM((2, 3, tokens, cols), jnp.bfloat16), xs],
         name='second',
         **settings,
-    )(*args, *parts)
+    )(*args, partial)
 
 
 def out_kernel(y_refs_per_half, a_ref, w_ref, *refs):
@@ -277,8 +286,7 @@
         theirs = lax.ppermute(jnp.stack([code.astype(jnp.float32), gate_vals]), 'ep', swap)
         flat = (num_micro, tokens, -1)
         first = me * slots
-        w_own = gates(code.reshape(flat) - first, gate_vals.reshape(flat), slots, norm_w)
-        w_their = gates(theirs[0].astype(jnp.int32).reshape(flat) - first, theirs[1].reshape(flat), slots, w_own)
+        w_their = gates(theirs[0].astype(jnp.int32).reshape(flat) - first, theirs[1].reshape(flat), slots, norm_w)
         flat_h = residual.reshape(num_micro * tokens, d_model)
         arrived, squares, after = [], 0.0, w_their
         for c in range(HALVES):
@@ -287,6 +295,8 @@
                 part, = mix(expert_out, m, c, 1 - me, w_their, after)
                 got.append(lax.ppermute(part, 'ep', swap))
                 after = part
+            if c == 0:
+                w_own = gates(code.reshape(flat) - first, gate_vals.reshape(flat), slots, after)
             ys, sums = [], []
             for m in range(num_micro):
                 after, total = mix(expert_out, m, c, me, w_own, after, (flat_h, got[m]))
@@ -298,10 +308,10 @@
         inv_rms = lax.rsqrt(squares.reshape(-1, 1) / d_model + NORM_EPS)
         inv_rms = jnp.broadcast_to(inv_rms, (num_micro * tokens, 128))
         weights = (w_query[0], w_key[0], w_value[0])
-        out = None
+        partial = None
         for c in range(HALVES):
-            out = project(c, arrived[c], inv_rms, norm_w, weights, out, seq_len)
-        result = project_out(out, w_out[0].reshape(-1, d_model), arrived)
+            partial = project(c, arrived[c], inv_rms, norm_w, weights, partial, seq_len)
+        result = project_out(partial, w_out[0].reshape(-1, d_model), arrived)
         return result.reshape(num_micro, seqs_dev, seq_len, d_model)
 
     return jax.shard_map(step, mesh=mesh, in_specs=(tok_spec, tok_spec, tok_spec, tok_spec, tok_spec, P('pp', None), wt_spec, wt_spec, wt_spec, wt_spec), out_specs=tok_spec, check_vma=False)

time: 351 us -> 327 us (0.932)
  Pallas kernels: 307 us -> 282 us
  waiting for transfers between devices: 20.6 us -> 27.3 us
  local copies, waits for them, and re-layouts: 11.1 us -> 4.93 us
    pallas_call x8, Pallas kernels: 72.6 us -> 61.8 us  [mix(): pl.pallas_call(functools.partial(mix_kernel, add is not None), out_shape=...]
    pallas_call x1, Pallas kernels: 82.3 us -> 71.9 us  [project(): pl.pallas_call(first_kernel, out_shape=jax.ShapeDtypeStruct((3, tokens, h...]
    ppermute x1, waiting for transfers between devices: 20.5 us -> 26.5 us  [step(): squares = lax.ppermute(squares, 'pp', send_next)]
    pallas_call x2, Pallas kernels: 11.9 us -> 7.13 us  [gates(): pl.pallas_call(gates_kernel, out_shape=jax.ShapeDtypeStruct((rows, 3 * to...]
  transfers between devices with their start and end apart: 10 -> 10, of which waited for: 1 -> 2; matrix products, arithmetic and copies ran while one was open for 2% -> 1% of each run, Pallas kernels for 38% -> 35%
where the time goes in v4:
time: 327 us; the launch traced here: 326 us
  Pallas kernels  282 us (86%)
  waiting for transfers between devices  27.3 us (8%)
  starting transfers between devices  9.71 us (3%)
  local copies, waits for them, and re-layouts  4.93 us (2%)
    pallas_call x1, Pallas kernels, project(): pl.pallas_call(functools.partial(second_kernel, seq_len, head_dim), out_s...  97.1 us
    pallas_call x1, Pallas kernels, project(): pl.pallas_call(first_kernel, out_shape=jax.ShapeDtypeStruct((3, tokens, h...  71.9 us
    pallas_call x8, Pallas kernels, mix(): pl.pallas_call(functools.partial(mix_kernel, add is not None), out_shape=...  61.8 us
    pallas_call x1, Pallas kernels, project_out(): pl.pallas_call(functools.partial(out_kernel, len(ys[0])), out_shape=jax.S...  44.3 us
    ppermute x1, waiting for transfers between devices, step(): squares = lax.ppermute(squares, 'pp', send_next)  26.5 us
    pallas_call x2, Pallas kernels, gates(): pl.pallas_call(gates_kernel, out_shape=jax.ShapeDtypeStruct((rows, 3 * to...  7.13 us
  transfers between devices with their start and end apart: 10, of which 2 were waited for; matrix products, arithmetic and copies ran while one was open for 1% of the time, Pallas kernels for 35%

profile of v4, /device:TPU:0, one launch (start us, length us, event | category | flops | bytes accessed | tf_op | source)
XLA Modules:
  0.0 326.1 jit_solution(11175969066151959815)
XLA Ops:
  0.0 0.7 convert_bitcast_fusion
  0.7 0.7 pad_maximum_fusion
  1.5 0.8 collective-permute-start
  2.3 0.9 collective-permute-done
  3.2 0.1 copy.18
  3.3 0.1 copy.17
  3.4 0.0 copy-start.2
  3.5 0.7 copy-done.2
  4.2 3.6 %gates.2.w_ref.after_ref = bf16[2,768,1536]{2,1,0:T(8,128)(2,1)S(1)} custom-call(s32[2,256,8]{2,1,0:T(8,128)S(1)} %bitcast.30, f32[2,256,8]{2,1,0:T(8,128)S(1)} %bitcast.28, f32[1,4096]{1,0:T(1,128)S(1)} %copy-done.2), custom_call_target="tpu_custom_call" | custom-call | flops 50331648 | bytes 4718592 | tf_op jit(solution)/shard_map/gates/pallas_call | solution.py:37
  7.7 0.0 copy-start
  7.7 9.3 %shard_map.100.after_ref = f32[256,2048]{1,0:T(8,128)} custom-call(s32[1]{0:T(128)} %bitcast.3.side_ref, bf16[2,768,1536]{2,1,0:T(8,128)(2,1)S(1)} %gates.2.w_ref.after_ref, bf16[2,64,48,4096]{3,2,1,0:T(8,128)(2,1)} %exp_ref.15, bf16[2,768,1536]{2,1,0:T(8,128)(2,1)S(1)} %gates.2.w_ref.after_ref), custom_call_target="tpu_custom_call" | custom-call | flops 4831838208 | bytes 6291456 | tf_op jit(solution)/shard_map/pallas_call | solution.py:98
  17.1 0.0 copy-start.7
  17.1 0.3 collective-permute-start.1
  17.4 0.0 copy-done
  17.4 7.2 %shard_map.101.after_ref = f32[256,2048]{1,0:T(8,128)S(1)} custom-call(s32[1]{0:T(128)} %bitcast.3.side_ref, bf16[2,768,1536]{2,1,0:T(8,128)(2,1)S(1)} %gates.2.w_ref.after_ref, bf16[2,64,48,4096]{3,2,1,0:T(8,128)(2,1)} %exp_ref.15, f32[256,2048]{1,0:T(8,128)} %shard_map.100.after_ref), custom_call_target="tpu_custom_call" | custom-call | flops 4831838208 | bytes 6291456 | tf_op jit(solution)/shard_map/pallas_call | solution.py:98
  24.6 0.2 collective-permute-start.2
  24.8 0.0 copy-done.7
  24.8 0.1 copy.16
  24.9 0.1 copy.15
  25.0 0.0 copy-start.1
  25.0 0.0 slice-start
  25.0 3.6 %gates.3.w_ref = bf16[2,768,1536]{2,1,0:T(8,128)(2,1)S(1)} custom-call(s32[2,256,8]{2,1,0:T(8,128)S(1)} %bitcast.31, f32[2,256,8]{2,1,0:T(8,128)S(1)} %bitcast.29, f32[256,2048]{1,0:T(8,128)S(1)} %shard_map.101.after_ref), custom_call_target="tpu_custom_call" | custom-call | flops 50331648 | bytes 4718592 | tf_op jit(solution)/shard_map/gates/pallas_call | solution.py:37
  28.6 0.0 collective-permute-done.1.rest_1_
  28.6 0.0 copy-done.1
  28.6 0.0 slice-start.1
  28.7 7.8 %shard_map.102 = (bf16[256,2048]{1,0:T(8,128)(2,1)S(1)}, f32[256,128]{1,0:T(8,128)S(1)}) custom-call(s32[1]{0:T(128)} %bitcast.side_ref, bf16[2,768,1536]{2,1,0:T(8,128)(2,1)S(1)} %gates.3.w_ref, bf16[2,64,48,4096]{3,2,1,0:T(8,128)(2,1)} %exp_ref.15, f32[256,2048]{1,0:T(8,128)S(1)} %shard_map.101.after_ref, bf16[512,4096]{1,0:T(8,128)(2,1)S(1)} %bitcast.24, ...), custom_call_target="tpu_custom_call" | custom-call | flops 4831838208 | bytes 6291456 | tf_op jit(solution)/shard_map/pallas_call | solution.py:98
  36.4 0.0 collective-permute-done.2.rest_1_
  36.4 7.7 %shard_map.103 = (bf16[256,2048]{1,0:T(8,128)(2,1)S(1)}, f32[256,128]{1,0:T(8,128)S(1)}) custom-call(s32[1]{0:T(128)} %bitcast.side_ref, bf16[2,768,1536]{2,1,0:T(8,128)(2,1)S(1)} %gates.3.w_ref, bf16[2,64,48,4096]{3,2,1,0:T(8,128)(2,1)} %exp_ref.15, bf16[256,2048]{1,0:T(8,128)(2,1)S(1)} %get-tuple-element.13.after_ref, bf16[512,4096]{1,0:T(8,128)(2,1)S(1)} %bitcast.25, ...), custom_call_target="tpu_custom_call" | custom-call | flops 4831838208 | bytes 6291456 | tf_op jit(solution)/shard_map/pallas_call | solution.py:98
  44.2 0.0 slice-done
  44.2 0.0 slice-done.1
  44.2 7.2 %shard_map.104.after_ref = f32[256,2048]{1,0:T(8,128)S(1)} custom-call(s32[1]{0:T(128)} %bitcast.3.side_ref, bf16[2,768,1536]{2,1,0:T(8,128)(2,1)S(1)} %bitcast.23, bf16[2,64,48,4096]{3,2,1,0:T(8,128)(2,1)} %exp_ref.15, bf16[256,2048]{1,0:T(8,128)(2,1)S(1)} %get-tuple-element.14.after_ref), custom_call_target="tpu_custom_call" | custom-call | flops 4831838208 | bytes 6291456 | tf_op jit(solution)/shard_map/pallas_call | solution.py:98
  51.4 0.4 collective-permute-start.3
  51.8 7.2 %shard_map.105.after_ref = f32[256,2048]{1,0:T(8,128)S(1)} custom-call(s32[1]{0:T(128)} %bitcast.3.side_ref, bf16[2,768,1536]{2,1,0:T(8,128)(2,1)S(1)} %bitcast.23, bf16[2,64,48,4096]{3,2,1,0:T(8,128)(2,1)} %exp_ref.15, f32[256,2048]{1,0:T(8,128)S(1)} %shard_map.104.after_ref), custom_call_target="tpu_custom_call" | custom-call | flops 4831838208 | bytes 6291456 | tf_op jit(solution)/shard_map/pallas_call | solution.py:98
  59.0 0.1 collective-permute-start.5
  59.1 2.8 collective-permute-start.9
  61.9 1.5 collective-permute-start.8
  63.4 0.1 slice_reduce_fusion.3
  63.5 0.1 slice_reduce_fusion.2
  63.6 0.0 collective-permute-done.3.rest_1_
  63.6 7.8 %shard_map.106 = (bf16[256,2048]{1,0:T(8,128)(2,1)S(1)}, f32[256,128]{1,0:T(8,128)S(1)}) custom-call(s32[1]{0:T(128)} %bitcast.side_ref, bf16[2,768,1536]{2,1,0:T(8,128)(2,1)S(1)} %gates.3.w_ref, bf16[2,64,48,4096]{3,2,1,0:T(8,128)(2,1)} %exp_ref.15, f32[256,2048]{1,0:T(8,128)S(1)} %shard_map.105.after_ref, bf16[512,4096]{1,0:T(8,128)(2,1)S(1)} %bitcast.26, ...), custom_call_target="tpu_custom_call" | custom-call | flops 4831838208 | bytes 6291456 | tf_op jit(solution)/shard_map/pallas_call | solution.py:98
  71.4 0.1 slice_reduce_fusion.1
  71.5 0.0 collective-permute-done.5.rest_1_
  71.5 7.8 %shard_map.107 = (bf16[256,2048]{1,0:T(8,128)(2,1)S(1)}, f32[256,128]{1,0:T(8,128)S(1)}) custom-call(s32[1]{0:T(128)} %bitcast.side_ref, bf16[2,768,1536]{2,1,0:T(8,128)(2,1)S(1)} %gates.3.w_ref, bf16[2,64,48,4096]{3,2,1,0:T(8,128)(2,1)} %exp_ref.15, bf16[256,2048]{1,0:T(8,128)(2,1)S(1)} %get-tuple-element.15.after_ref, bf16[512,4096]{1,0:T(8,128)(2,1)S(1)} %bitcast.27, ...), custom_call_target="tpu_custom_call" | custom-call | flops 4831838208 | bytes 6291456 | tf_op jit(solution)/shard_map/pallas_call | solution.py:98
  79.3 0.1 slice_reduce_fusion
  79.5 1.5 collective-permute-start.7
  81.0 0.0 collective-permute-start.4
  81.0 1.9 collective-permute-start.6
  82.9 26.5 %collective-permute-done.7 = f32[2,256]{1,0:T(2,128)S(1)} collective-permute-done((f32[2,256]{1,0:T(2,128)S(1)}, f32[2,256]{1,0:T(2,128)S(1)}, u32[]{:S(2)}, u32[]{:S(2)}) %collective-permute-start.7) | collective-permute-done | bytes 2080 | tf_op jit(solution)/shard_map/ppermute | solution.py:307
  109.4 0.0 collective-permute-done.9.y1_ref.refs_1_
  109.4 0.0 copy-start.3
  109.4 0.0 collective-permute-done.8.y0_ref.refs_0_
  109.4 0.0 copy-start.4
  109.4 1.0 broadcast_in_dim.10.inv_ref
  110.5 0.1 copy-done.3
  110.5 0.3 copy-done.4
  110.8 71.9 %first.1.refs_3_ = f32[3,512,8192]{2,1,0:T(8,128)} custom-call(bf16[256,2048]{1,0:T(8,128)(2,1)} %copy-done.4, bf16[256,2048]{1,0:T(8,128)(2,1)} %copy-done.3, f32[512,128]{1,0:T(8,128)} %broadcast_in_dim.10.inv_ref, f32[1,4096]{1,0:T(1,128)} %norm_ref.3, bf16[4096,64,128]{2,1,0:T(8,128)(2,1)} %bitcast.9.refs_0_, bf16[4096,64,128]{2,1,0:T(8,128)(2,1)} %bitcast.10.refs_1_, ...), custom_call_target="tpu_custom_call" | custom-call | flops 51539607552 | bytes 100663296 | tf_op jit(solution)/shard_map/first/pallas_call | solution.py:212
  182.8 0.0 collective-permute-done.6.y1_ref.refs_3_
  182.8 0.0 copy-start.6
  182.8 0.0 collective-permute-done.4.y0_ref.refs_2_
  182.8 0.9 copy-done.6
  183.7 0.0 copy-start.5
  183.7 1.0 copy-done.5
  184.7 97.1 %second.1.a_ref = bf16[512,8192]{1,0:T(8,128)(2,1)} custom-call(bf16[256,2048]{1,0:T(8,128)(2,1)} %copy-done.5, bf16[256,2048]{1,0:T(8,128)(2,1)} %copy-done.6, f32[512,128]{1,0:T(8,128)} %broadcast_in_dim.10.inv_ref, f32[1,4096]{1,0:T(1,128)} %norm_ref.3, bf16[4096,64,128]{2,1,0:T(8,128)(2,1)} %bitcast.9.refs_0_, bf16[4096,64,128]{2,1,0:T(8,128)(2,1)} %bitcast.10.refs_1_, ...), custom_call_target="tpu_custom_call" | custom-call | flops 51539607552 | bytes 100663296 | tf_op jit(solution)/shard_map/second/pallas_call | solution.py:222
  281.8 44.3 %out.1 = bf16[512,4096]{1,0:T(8,128)(2,1)} custom-call(bf16[512,8192]{1,0:T(8,128)(2,1)} %second.1.a_ref, bf16[8192,4096]{1,0:T(8,128)(2,1)} %bitcast.12.w_ref, bf16[256,2048]{1,0:T(8,128)(2,1)} %copy-done.4, bf16[256,2048]{1,0:T(8,128)(2,1)} %copy-done.3, bf16[256,2048]{1,0:T(8,128)(2,1)} %copy-done.5, bf16[256,2048]{1,0:T(8,128)(2,1)} %copy-done.6), custom_call_target="tpu_custom_call" | custom-call | flops 34359738368 | bytes 67108864 | tf_op jit(solution)/shard_map/out/pallas_call | solution.py:259
  (6 shorter events, 0.0 us)
Async XLA Ops:
  1.5 1.7 collective-permute-start
  3.4 0.7 copy-start.2
  7.7 9.7 %copy-start = (bf16[2,768,1536]{2,1,0:T(8,128)(2,1)}, bf16[2,768,1536]{2,1,0:T(8,128)(2,1)S(1)}, u32[]{:S(2)}) copy-start(bf16[2,768,1536]{2,1,0:T(8,128)(2,1)S(1)} %gates.2.w_ref.after_ref) | copy-start | bytes 14155780
  17.1 7.7 %copy-start.7 = (f32[2,2,128,8]{2,3,1,0:T(8,128)S(1)}, f32[2,2,128,8]{2,3,1,0:T(8,128)}, u32[]{:S(2)}) copy-start(f32[2,2,128,8]{2,3,1,0:T(8,128)} %param.13) | copy-start | bytes 49156
  17.1 11.6 %collective-permute-start.1 = (f32[256,2048]{1,0:T(8,128)}, f32[256,2048]{1,0:T(8,128)}, u32[]{:S(2)}, u32[]{:S(2)}) collective-permute-start(f32[256,2048]{1,0:T(8,128)} %shard_map.100.after_ref), channel_id=1, source_target_pairs={{0,1},{1,0},{2,3},{3,2},{4,5},{5,4},{6,7},{7,6}} | collective-permute-start | bytes 6291464 | tf_op jit(solution)/shard_map/ppermute | solution.py:296
  24.6 11.9 %collective-permute-start.2 = (f32[256,2048]{1,0:T(8,128)S(1)}, f32[256,2048]{1,0:T(8,128)}, u32[]{:S(2)}, u32[]{:S(2)}) collective-permute-start(f32[256,2048]{1,0:T(8,128)S(1)} %shard_map.101.after_ref), channel_id=1, source_target_pairs={{0,1},{1,0},{2,3},{3,2},{4,5},{5,4},{6,7},{7,6}} | collective-permute-start | bytes 6291464 | tf_op jit(solution)/shard_map/ppermute | solution.py:296
  25.0 3.6 %copy-start.1 = (bf16[2,2,128,4096]{3,2,1,0:T(8,128)(2,1)S(1)}, bf16[2,2,128,4096]{3,2,1,0:T(8,128)(2,1)}, u32[]{:S(2)}) copy-start(bf16[2,2,128,4096]{3,2,1,0:T(8,128)(2,1)} %param.14) | copy-start | bytes 12582916
  25.0 19.1 %slice-start = ((s8[4718592]{0:T(1024)(128)(4,1)}), s8[4194304]{0:T(1024)(128)(4,1)S(1)}, s32[]{:S(2)}) async-start(s8[4718592]{0:T(1024)(128)(4,1)} %bitcast.22), calls=%async_computation | async-start | bytes 8388608
  28.6 15.5 %slice-start.1 = ((s8[4718592]{0:T(1024)(128)(4,1)}), s8[524288]{0:T(1024)(128)(4,1)S(1)}, s32[]{:S(2)}) async-start(s8[4718592]{0:T(1024)(128)(4,1)} %bitcast.22), calls=%async_computation.1 | async-start | bytes 1048576
  51.4 12.2 %collective-permute-start.3 = (f32[256,2048]{1,0:T(8,128)S(1)}, f32[256,2048]{1,0:T(8,128)S(1)}, u32[]{:S(2)}, u32[]{:S(2)}) collective-permute-start(f32[256,2048]{1,0:T(8,128)S(1)} %shard_map.104.after_ref), channel_id=1, source_target_pairs={{0,1},{1,0},{2,3},{3,2},{4,5},{5,4},{6,7},{7,6}} | collective-permute-start | bytes 6291464 | tf_op jit(solution)/shard_map/ppermute | solution.py:296
  59.0 12.5 %collective-permute-start.5 = (f32[256,2048]{1,0:T(8,128)S(1)}, f32[256,2048]{1,0:T(8,128)S(1)}, u32[]{:S(2)}, u32[]{:S(2)}) collective-permute-start(f32[256,2048]{1,0:T(8,128)S(1)} %shard_map.105.after_ref), channel_id=1, source_target_pairs={{0,1},{1,0},{2,3},{3,2},{4,5},{5,4},{6,7},{7,6}} | collective-permute-start | bytes 6291464 | tf_op jit(solution)/shard_map/ppermute | solution.py:296
  59.1 50.3 %collective-permute-start.9 = (bf16[256,2048]{1,0:T(8,128)(2,1)S(1)}, bf16[256,2048]{1,0:T(8,128)(2,1)S(1)}, u32[]{:S(2)}, u32[]{:S(2)}) collective-permute-start(bf16[256,2048]{1,0:T(8,128)(2,1)S(1)} %get-tuple-element.14.after_ref), channel_id=1, source_target_pairs={{0,2},{2,4},{4,6},{6,0},{1,3},{3,5},{5,7},{7,1}} | collective-permute-start | bytes 3145736 | tf_op jit(solution)/shard_map/ppermute | solution.py:304
  61.9 47.5 %collective-permute-start.8 = (bf16[256,2048]{1,0:T(8,128)(2,1)S(1)}, bf16[256,2048]{1,0:T(8,128)(2,1)S(1)}, u32[]{:S(2)}, u32[]{:S(2)}) collective-permute-start(bf16[256,2048]{1,0:T(8,128)(2,1)S(1)} %get-tuple-element.13.after_ref), channel_id=1, source_target_pairs={{0,2},{2,4},{4,6},{6,0},{1,3},{3,5},{5,7},{7,1}} | collective-permute-start | bytes 3145736 | tf_op jit(solution)/shard_map/ppermute | solution.py:304
  79.5 29.9 %collective-permute-start.7 = (f32[2,256]{1,0:T(2,128)S(1)}, f32[2,256]{1,0:T(2,128)S(1)}, u32[]{:S(2)}, u32[]{:S(2)}) collective-permute-start(f32[2,256]{1,0:T(2,128)S(1)} %maximum_add_fusion), channel_id=1, source_target_pairs={{0,2},{2,4},{4,6},{6,0},{1,3},{3,5},{5,7},{7,1}} | collective-permute-start | bytes 6152 | tf_op jit(solution)/shard_map/ppermute | solution.py:307
  81.0 101.8 %collective-permute-start.4 = (bf16[256,2048]{1,0:T(8,128)(2,1)S(1)}, bf16[256,2048]{1,0:T(8,128)(2,1)S(1)}, u32[]{:S(2)}, u32[]{:S(2)}) collective-permute-start(bf16[256,2048]{1,0:T(8,128)(2,1)S(1)} %get-tuple-element.15.after_ref), channel_id=1, source_target_pairs={{0,2},{2,4},{4,6},{6,0},{1,3},{3,5},{5,7},{7,1}} | collective-permute-start | bytes 3145736 | tf_op jit(solution)/shard_map/ppermute | solution.py:304
  81.0 101.8 %collective-permute-start.6 = (bf16[256,2048]{1,0:T(8,128)(2,1)S(1)}, bf16[256,2048]{1,0:T(8,128)(2,1)S(1)}, u32[]{:S(2)}, u32[]{:S(2)}) collective-permute-start(bf16[256,2048]{1,0:T(8,128)(2,1)S(1)} %get-tuple-element.16), channel_id=1, source_target_pairs={{0,2},{2,4},{4,6},{6,0},{1,3},{3,5},{5,7},{7,1}} | collective-permute-start | bytes 3145736 | tf_op jit(solution)/shard_map/ppermute | solution.py:304
  109.4 1.1 copy-start.3
  109.4 1.4 copy-start.4
  182.8 0.9 copy-start.6
  183.7 1.0 copy-start.5
